TPU v7x, 128 devices: a whole 4x4x4 slice. The times are simulated.
128 devices in a mesh: seq: 32 (over z, y_hi, x), head: 4 (over y_lo, core).
Axes of the slice: x: 4, y: 4 (y_hi: 2, y_lo: 2; y = y_hi * 2 + y_lo), z: 4, core: 2. Of those that a mesh axis runs over, the one named last changes fastest.
Arguments:
- queries: bfloat16 [8192, 3584], P('seq', 'head'), may hold values from -5 to 5
- keys: bfloat16 [8192, 3584], P('seq', 'head'), may hold values from -5 to 5
- values: bfloat16 [8192, 3584], P('seq', 'head'), may hold values from -6 to 6
- attn_grad: bfloat16 [8192, 3584], P('seq', 'head'), may hold values from -6 to 6
- doc_ids: int32 [8192], replicated, may hold values from 0 to 7, never falling along the last dimension, each value on 1 to 4096 neighbouring positions
- conv_input: bfloat16 [8192, 7168], P('seq', 'head'), may hold values from -6 to 6
- conv_weight: float32 [4, 7168], P(None, 'head'), may hold values from -3 to 3
- step_raw: float32 [8192, 112], P('seq', 'head'), may hold values from -4 to 4
- step_bias: float32 [112], P('head'), may hold values from -1.5 to 0
- rate_log: float32 [112], P('head'), may hold values from -13 to -1
- skip_gain: float32 [112], P('head'), may hold values from 0.5 to 1.5
- input_coeff: bfloat16 [8192, 128], P('seq'), may hold values from -0.625 to 0.625
- output_coeff: bfloat16 [8192, 128], P('seq'), may hold values from -0.625 to 0.625
- gate_input: bfloat16 [8192, 7168], P('seq', 'head'), may hold values from -6 to 6
- mix_grad: bfloat16 [8192, 7168], P('seq', 'head'), may hold values from -1.5 to 1.5
Outputs:
- grad_queries: bfloat16 [8192, 3584], P('seq', 'head')
- grad_keys: bfloat16 [8192, 3584], P('seq', 'head')
- grad_values: bfloat16 [8192, 3584], P('seq', 'head')
- grad_conv_input: bfloat16 [8192, 7168], P('seq', 'head')
- grad_gate: bfloat16 [8192, 7168], P('seq', 'head')
- grad_step: float32 [8192, 112], P('seq', 'head')
- grad_input_coeff: float32 [8192, 128], P('seq')
- grad_output_coeff: float32 [8192, 128], P('seq')
- grad_conv_weight: float32 [4, 7168], P(None, 'head')
- grad_step_bias: float32 [112], P('head')
- grad_rate_log: float32 [112], P('head')
- grad_skip: float32 [112], P('head')
Inputs may be any that keep to these rules, and one draw needn't show every extreme that they name: doc_ids never fall along the sequence.
All inputs are finite; a program needn't handle non-finite values.
Results may differ from a plain program's by a relative error of at most 0.012.
Values may be sent and summed in bfloat16 or wider, within the bound.
A program may use at most 128 MiB of HBM per device.

v0:
```python
import functools

import jax
import jax.numpy as jnp
from jax import lax
from jax.experimental import pallas as pl
from jax.experimental.pallas import tpu as pltpu
from jax.sharding import PartitionSpec as P

HEAD_DIM = 224
WINDOW = 1024
SSM_HEADS = 112
STATE = 64
GROUPS = 2
T = 256
NH = 28
PAIRS = 14
NSEQ = 32
RING = 4
NEG = -1e30
F32 = jnp.float32
BF16 = jnp.bfloat16
MESH = pl.DeviceIdType.MESH
VM = pltpu.VMEM
SCALE = HEAD_DIM ** (-0.5)
HI = lax.Precision.HIGHEST


def dot(a, b, ca, cb, precision=None):
    return lax.dot_general(
        a, b, (((ca,), (cb,)), ((), ())), preferred_element_type=F32, precision=precision
    )


def sigmoid(v):
    return 1.0 / (1.0 + jnp.exp(-v))


def col_of(row, rows):
    return jnp.transpose(jnp.broadcast_to(row, (rows, row.shape[1])))


def prep_kernel(q_ref, k_ref, v_ref, g_ref, *refs):
    kv, qd, scr = refs[:4], refs[4:8], refs[8]
    x = lax.rem(lax.axis_index("seq"), RING)
    for slot, (src, dest) in enumerate(((k_ref, kv), (v_ref, kv), (q_ref, qd), (g_ref, qd))):
        scr[...] = jnp.transpose(src[...].astype(F32)).astype(BF16)
        for k in range(RING):
            h = lax.rem(x + k, RING)
            dest[k][slot % 2] = scr[pl.ds(pl.multiple_of(h * HEAD_DIM, 32), HEAD_DIM), :]


def attn_prep(queries, keys, values, attn_grad):
    piece = jax.ShapeDtypeStruct((2, HEAD_DIM, T), BF16)
    return pl.pallas_call(
        prep_kernel,
        out_shape=[piece] * 8,
        scratch_shapes=[VM((4 * HEAD_DIM, T), BF16)],
        name="attn_prep",
        cost_estimate=pl.CostEstimate(flops=4000000, bytes_accessed=4000000, transcendentals=0),
    )(queries, keys, values, attn_grad)


def attn_kernel(*refs):
    kv, qd, halo, doc_ref = refs[0:4], refs[4:8], refs[8:12], refs[12]
    own, back = refs[13:17], refs[17:21]
    akv, aqd, dka, dva, doq = refs[21:26]
    x = lax.rem(lax.axis_index("seq"), RING)
    for k in range(RING):
        c = lax.rem(x - k + RING, RING)
        akv[RING + c] = kv[k][...]
        akv[c] = halo[k][...]
        aqd[c] = qd[k][...]
    dka[...] = jnp.zeros_like(dka)
    dva[...] = jnp.zeros_like(dva)
    row_i = lax.broadcasted_iota(jnp.int32, (T, T), 0)
    col_j = lax.broadcasted_iota(jnp.int32, (T, T), 1)

    def chunk(c, carry):
        qt = aqd[c, 0]
        gt = aqd[c, 1]
        q = jnp.transpose(qt.astype(F32)).astype(BF16)
        g = jnp.transpose(gt.astype(F32)).astype(BF16)
        dq_col = col_of(doc_ref[pl.ds(RING + c, 1), :], 128)
        dq_col = jnp.concatenate([dq_col, dq_col], axis=1)
        scores, masks = [], []
        row_max = None
        for b in range(RING + 1):
            s = dot(q, akv[c + b, 0], 1, 0) * SCALE
            ok = dq_col == doc_ref[pl.ds(c + b, 1), :]
            if b == 0:
                ok = ok & (col_j > row_i)
            if b == RING:
                ok = ok & (col_j <= row_i)
            s = jnp.where(ok, s, NEG)
            scores.append(s)
            masks.append(ok)
            m = jnp.max(s, axis=1, keepdims=True)
            row_max = m if row_max is None else jnp.maximum(row_max, m)
        row_sum = None
        for b in range(RING + 1):
            e = jnp.where(masks[b], jnp.exp(scores[b] - row_max), 0.0)
            scores[b] = e
            r = jnp.sum(e, axis=1, keepdims=True)
            row_sum = r if row_sum is None else row_sum + r
        inv = 1.0 / jnp.maximum(row_sum, 1.0)
        dprobs = []
        delta = None
        for b in range(RING + 1):
            p = scores[b] * inv
            scores[b] = p
            half = p.astype(BF16)
            dp = dot(g, akv[c + b, 1], 1, 0)
            dprobs.append(dp)
            r = jnp.sum(half.astype(F32) * dp, axis=1, keepdims=True)
            delta = r if delta is None else delta + r
            dva[c + b] = dva[c + b] + dot(gt, half, 1, 0)
        dqt = None
        for b in range(RING + 1):
            ds = (scores[b] * (dprobs[b] - delta)).astype(BF16)
            r = dot(akv[c + b, 0], ds, 1, 1)
            dqt = r if dqt is None else dqt + r
            dka[c + b] = dka[c + b] + dot(qt, ds, 1, 0)
        doq[c] = dqt
        return carry

    lax.fori_loop(0, RING, chunk, 0)
    for k in range(RING):
        c = lax.rem(x + k, RING)
        own[k][0] = (doq[c] * SCALE).astype(BF16)
        own[k][1] = (dka[RING + c] * SCALE).astype(BF16)
        own[k][2] = dva[RING + c].astype(BF16)
        back[k][0] = (dka[c] * SCALE).astype(BF16)
        back[k][1] = dva[c].astype(BF16)


def attn_core(kv, qd, halo, doc_rows):
    return pl.pallas_call(
        attn_kernel,
        out_shape=[jax.ShapeDtypeStruct((3, HEAD_DIM, T), BF16)] * 4
        + [jax.ShapeDtypeStruct((2, HEAD_DIM, T), BF16)] * 4,
        scratch_shapes=[
            VM((2 * RING, 2, HEAD_DIM, T), BF16),
            VM((RING, 2, HEAD_DIM, T), BF16),
            VM((2 * RING, HEAD_DIM, T), F32),
            VM((2 * RING, HEAD_DIM, T), F32),
            VM((RING, HEAD_DIM, T), F32),
        ],
        name="attn_core",
        cost_estimate=pl.CostEstimate(
            flops=3000000000, bytes_accessed=8000000, transcendentals=1400000
        ),
    )(*kv, *qd, *halo, doc_rows)


def attn_final_kernel(*refs):
    own, back = refs[0:4], refs[4:8]
    dq_ref, dk_ref, dv_ref, scr = refs[8:12]
    x = lax.rem(lax.axis_index("seq"), RING)
    for slot, dest in enumerate((dq_ref, dk_ref, dv_ref)):
        for k in range(RING):
            h = lax.rem(x - k + RING, RING)
            part = own[k][slot].astype(F32)
            if slot:
                part = part + back[k][slot - 1].astype(F32)
            scr[pl.ds(pl.multiple_of(h * HEAD_DIM, 32), HEAD_DIM), :] = part
        dest[...] = jnp.transpose(scr[...]).astype(BF16)


def attn_final(own, back):
    whole = jax.ShapeDtypeStruct((T, 4 * HEAD_DIM), BF16)
    return pl.pallas_call(
        attn_final_kernel,
        out_shape=[whole] * 3,
        scratch_shapes=[VM((4 * HEAD_DIM, T), F32)],
        name="attn_final",
        cost_estimate=pl.CostEstimate(flops=4000000, bytes_accessed=4000000, transcendentals=0),
    )(*own, *back)


def ring_shift(value, k):
    if k == 0:
        return value
    return lax.ppermute(
        value, "seq", [(s, s // RING * RING + (s + k) % RING) for s in range(NSEQ)]
    )


def group_shift(value, k, step):
    pairs = []
    for s in range(NSEQ):
        group, x = divmod(s, RING)
        if 0 <= group + step < NSEQ // RING:
            pairs.append((s, (group + step) * RING + (x + k) % RING))
    return lax.ppermute(value, "seq", pairs)


def mixer_setup(raw_ref, bias_ref, rate_ref, docc_ref, rows, tri, scr, mk):
    scr[...] = jnp.zeros_like(scr)
    step = jnp.log(1.0 + jnp.exp(raw_ref[...] + bias_ref[...]))
    scr[:, 0:NH] = step
    rows[0] = jnp.transpose(scr[...])[0:32]
    scr[:, 0:NH] = -step * jnp.exp(rate_ref[...])
    ld = jnp.transpose(scr[...])[0:32]
    rows[1] = ld
    i = lax.broadcasted_iota(jnp.int32, (T, T), 0)
    j = lax.broadcasted_iota(jnp.int32, (T, T), 1)
    tri[...] = jnp.where(i <= j, 1.0, 0.0)
    cum = dot(ld, tri[...], 1, 0, HI)
    rows[2] = cum
    rows[3] = jnp.where(docc_ref[1:2, :] > 0.0, jnp.exp(cum), 0.0)
    rows[4] = jnp.where(
        docc_ref[2:3, :] > 0.0, jnp.exp(jnp.minimum(cum[:, T - 1 : T] - cum, 0.0)), 0.0
    )
    for k in range(3):
        mk[k] = col_of(docc_ref[3 + k : 4 + k, :], 128)


def pair_rows(rows, which, pair):
    a = rows[which, pl.ds(2 * pair, 1), :]
    b = rows[which, pl.ds(2 * pair + 1, 1), :]
    return jnp.concatenate(
        [jnp.broadcast_to(a, (64, T)), jnp.broadcast_to(b, (64, T))], axis=0
    )


def group_cols(ref, group):
    v = ref[...].astype(F32)
    return jnp.where(group == 0, v[:, 0:STATE], v[:, STATE:])


def conv_forward(x, tail_ref, w_ref, mk, xs):
    xs[0:8, :] = tail_ref[...]
    xs[8 : 8 + T, :] = x
    pre = w_ref[0:1, :] * x
    for k in range(1, 4):
        pre = pre + w_ref[k : k + 1, :] * (mk[k - 1] * xs[8 - k : 8 - k + T, :])
    return pre


def phase_a_kernel(
    conv_ref, tail_ref, gate_ref, mix_ref, w_ref, raw_ref, bias_ref, rate_ref, docc_ref,
    bin_ref, cout_ref,
    act_out, g_out, loc_out, thr_out,
    rows, tri, scr, mk, xs, bg, cg,
):
    pair = pl.program_id(0)

    @pl.when(pair == 0)
    def _():
        mixer_setup(raw_ref, bias_ref, rate_ref, docc_ref, rows, tri, scr, mk)
        group = lax.axis_index("head") // 2
        bg[...] = group_cols(bin_ref, group).astype(BF16)
        cg[...] = group_cols(cout_ref, group).astype(BF16)
        thr = rows[3][:, T - 1 : T]
        thr_out[...] = jnp.broadcast_to(thr, (32, 128))

    x = conv_ref[...].astype(F32)
    pre = conv_forward(x, tail_ref, w_ref, mk, xs)
    act = pre * sigmoid(pre)
    gate = gate_ref[...].astype(F32)
    g = mix_ref[...].astype(F32) * (gate * sigmoid(gate))
    act_t = jnp.transpose(act)
    g_t = jnp.transpose(g)
    act_out[...] = act_t
    g_out[...] = g_t
    st = act_t * (pair_rows(rows, 0, pair) * pair_rows(rows, 4, pair))
    ge = g_t * pair_rows(rows, 3, pair)
    loc_out[:, 0:STATE] = dot(st.astype(BF16), bg[...], 1, 0).astype(BF16)
    loc_out[:, STATE:] = dot(ge.astype(BF16), cg[...], 1, 0).astype(BF16)


def whole_spec(shape):
    return pl.BlockSpec(shape, lambda i: (0,) * len(shape))


def phase_a(conv_input, tail8, gate_input, mix_grad, conv_weight, raw, bias, rate, docc, bin_, cout):
    tok = pl.BlockSpec((T, 128), lambda i: (0, i))
    chan = pl.BlockSpec((128, T), lambda i: (i, 0))
    return pl.pallas_call(
        phase_a_kernel,
        grid=(PAIRS,),
        in_specs=[
            tok,
            pl.BlockSpec((8, 128), lambda i: (0, i)),
            tok,
            tok,
            pl.BlockSpec((4, 128), lambda i: (0, i)),
            whole_spec((T, NH)),
            whole_spec((1, NH)),
            whole_spec((1, NH)),
            whole_spec((8, T)),
            whole_spec((T, 128)),
            whole_spec((T, 128)),
        ],
        out_specs=[
            chan,
            chan,
            pl.BlockSpec((128, 128), lambda i: (i, 0)),
            whole_spec((32, 128)),
        ],
        out_shape=[
            jax.ShapeDtypeStruct((NH * 64, T), F32),
            jax.ShapeDtypeStruct((NH * 64, T), F32),
            jax.ShapeDtypeStruct((NH * 64, 128), BF16),
            jax.ShapeDtypeStruct((32, 128), F32),
        ],
        scratch_shapes=[
            VM((5, 32, T), F32),
            VM((T, T), F32),
            VM((T, 128), F32),
            VM((3, T, 128), F32),
            VM((8 + T, 128), F32),
            VM((T, STATE), BF16),
            VM((T, STATE), BF16),
        ],
        name="mixer_a",
        cost_estimate=pl.CostEstimate(
            flops=600000000, bytes_accessed=7000000, transcendentals=1000000
        ),
    )(conv_input, tail8, gate_input, mix_grad, conv_weight, raw, bias, rate, docc, bin_, cout)


def phase_b_kernel(
    conv_ref, tail_ref, gate_ref, mix_ref, w_ref, raw_ref, bias_ref, rate_ref, docc_ref,
    bin_ref, cout_ref, act_ref, g_ref, st_ref, skip_ref,
    dconv_out, dgate_out, spill_out, last_out, red_out, step_out, scal_out, coef_out,
    rows, tri, scr, mk, xs, bg, cg, cgt, bias_m, pair_t, dpair, dcum, ddir, dskp, dbt, dct, qs,
):
    pair = pl.program_id(0)

    @pl.when(pair == 0)
    def _():
        mixer_setup(raw_ref, bias_ref, rate_ref, docc_ref, rows, tri, scr, mk)
        group = lax.axis_index("head") // 2
        bf = group_cols(bin_ref, group)
        cf = group_cols(cout_ref, group)
        bg[...] = bf.astype(BF16)
        cg[...] = cf.astype(BF16)
        pair_t[...] = dot(bf, cf, 1, 1, HI)
        doc = docc_ref[0:1, :]
        dcol = col_of(doc, 128)
        dcol = jnp.concatenate([dcol, dcol], axis=1)
        ok = (tri[...] > 0.5) & (dcol == doc)
        bias_m[...] = jnp.where(ok, 0.0, NEG)
        dpair[...] = jnp.zeros_like(dpair)
        dbt[...] = jnp.zeros_like(dbt)
        dct[...] = jnp.zeros_like(dct)
        dcum[...] = jnp.zeros_like(dcum)
        ddir[...] = jnp.zeros_like(ddir)
        dskp[...] = jnp.zeros_like(dskp)
        qs[...] = jnp.zeros_like(qs)
        scal_out[...] = jnp.zeros_like(scal_out)

    act_t = act_ref[...]
    g_t = g_ref[...]
    step_p = pair_rows(rows, 0, pair)
    eg_p = pair_rows(rows, 3, pair)
    te_p = pair_rows(rows, 4, pair)
    s_t = act_t * step_p
    s_b = s_t.astype(BF16)
    g_b = g_t.astype(BF16)
    state = st_ref[...]
    start = state[:, 0:STATE]
    end = state[:, STATE:]
    car = dot(start, cg[...], 1, 1) * eg_p
    dste = dot(end, bg[...], 1, 1) * te_p
    dct[...] += dot(start, (g_t * eg_p).astype(BF16), 0, 0)
    dbt[...] += dot(end, (s_t * te_p).astype(BF16), 0, 0)
    se = start.astype(F32) * end.astype(F32)
    lane = lax.broadcasted_iota(jnp.int32, (1, T), 1)
    ys, dss = [], []
    for a in range(2):
        lo = 64 * a
        h = 2 * pair + a
        cum = rows[2, pl.ds(h, 1), :]
        cc = col_of(cum, 128)
        cc = jnp.concatenate([cc, cc], axis=1)
        w = jnp.exp(jnp.minimum(cum - cc, 0.0) + bias_m[...])
        m = pair_t[...] * w
        mb = m.astype(BF16)
        sh = s_b[lo : lo + 64]
        gh = g_b[lo : lo + 64]
        y = dot(sh, mb, 1, 0)
        dsi = dot(gh, mb, 1, 1)
        dm = dot(sh, gh, 0, 0)
        dpair[...] += dm * w
        z = dm * m
        zr = jnp.sum(jnp.transpose(z[:, 0:128] + z[:, 128:]), axis=0, keepdims=True)
        carh = car[lo : lo + 64]
        dsth = dste[lo : lo + 64]
        gt = g_t[lo : lo + 64]
        st = s_t[lo : lo + 64]
        at = act_t[lo : lo + 64]
        v = jnp.sum(st * dsth, axis=0, keepdims=True)
        d = jnp.sum(z, axis=0, keepdims=True) - zr + jnp.sum(gt * carh, axis=0, keepdims=True) - v
        thr = rows[3, pl.ds(h, 1), :][:, T - 1 : T]
        extra = jnp.sum(v, axis=1, keepdims=True) + thr * jnp.sum(
            jnp.sum(se[lo : lo + 64], axis=0, keepdims=True), axis=1, keepdims=True
        )
        dcum[pl.ds(h, 1), :] = d + jnp.where(lane == T - 1, extra, 0.0)
        ds = dsi + dsth
        ddir[pl.ds(h, 1), :] = jnp.sum(ds * at, axis=0, keepdims=True)
        dskp[pl.ds(h, 1), :] = jnp.sum(gt * at, axis=0, keepdims=True)
        skip = skip_ref[h]
        ys.append(y + carh + skip * at)
        dss.append(ds * step_p[lo : lo + 64] + skip * gt)
    y = jnp.transpose(jnp.concatenate(ys, axis=0))
    dact = jnp.transpose(jnp.concatenate(dss, axis=0))
    gate = gate_ref[...].astype(F32)
    sg = sigmoid(gate)
    dgate_out[...] = (
        mix_ref[...].astype(F32) * y * (sg * (1.0 + gate * (1.0 - sg)))
    ).astype(BF16)
    x = conv_ref[...].astype(F32)
    pre = conv_forward(x, tail_ref, w_ref, mk, xs)
    sp = sigmoid(pre)
    dpre = dact * (sp * (1.0 + pre * (1.0 - sp)))
    dx = None
    for k in range(4):
        q = dpre if k == 0 else dpre * mk[k - 1]
        red_out[0, k : k + 1, :] = jnp.sum(q * xs[8 - k : 8 - k + T, :], axis=0, keepdims=True)
        qs[8 : 8 + T, :] = q
        term = w_ref[k : k + 1, :] * qs[k : k + 8 + T, :]
        dx = term if dx is None else dx + term
    spill_out[...] = dx[0:8]
    dconv_out[...] = dx[8:].astype(BF16)
    last_out[...] = dx[T:]
    red_out[0, 4:8, :] = jnp.zeros((4, 128), F32)

    @pl.when(pair == PAIRS - 1)
    def _():
        dld = dot(dcum[...], tri[...], 1, 1, HI)
        zero = jnp.zeros((96, T), F32)
        to_tok = lambda v: jnp.transpose(jnp.concatenate([v, zero], axis=0))[:, 0:NH]
        dld_t = to_tok(dld)
        dir_t = to_tok(ddir[...])
        rate = jnp.exp(rate_ref[...])
        v = raw_ref[...] + bias_ref[...]
        step = jnp.log(1.0 + jnp.exp(v))
        gs = (dir_t - dld_t * rate) * sigmoid(v)
        step_out[...] = gs
        scal_out[0:1, 0:NH] = jnp.sum(gs, axis=0, keepdims=True)
        scal_out[1:2, 0:NH] = -rate * jnp.sum(dld_t * step, axis=0, keepdims=True)
        scal_out[2:3, 0:NH] = jnp.sum(to_tok(dskp[...]), axis=0, keepdims=True)
        dp = dpair[...].astype(BF16)
        coef_out[0:STATE] = (dbt[...] + dot(jnp.transpose(cg[...].astype(F32)).astype(BF16), dp, 1, 1)).astype(BF16)
        coef_out[STATE:] = (dct[...] + dot(jnp.transpose(bg[...].astype(F32)).astype(BF16), dp, 1, 0)).astype(BF16)


def phase_b(
    conv_input, tail8, gate_input, mix_grad, conv_weight, raw, bias, rate, docc, bin_, cout,
    act_t, g_t, states, skip,
):
    tok = pl.BlockSpec((T, 128), lambda i: (0, i))
    chan = pl.BlockSpec((128, T), lambda i: (i, 0))
    row8 = pl.BlockSpec((8, 128), lambda i: (0, i))
    width = NH * 64
    return pl.pallas_call(
        phase_b_kernel,
        grid=(PAIRS,),
        in_specs=[
            tok,
            row8,
            tok,
            tok,
            pl.BlockSpec((4, 128), lambda i: (0, i)),
            whole_spec((T, NH)),
            whole_spec((1, NH)),
            whole_spec((1, NH)),
            whole_spec((8, T)),
            whole_spec((T, 128)),
            whole_spec((T, 128)),
            chan,
            chan,
            pl.BlockSpec((128, 128), lambda i: (i, 0)),
            pl.BlockSpec(memory_space=pltpu.SMEM),
        ],
        out_specs=[
            tok,
            tok,
            row8,
            row8,
            pl.BlockSpec((1, 8, 128), lambda i: (i, 0, 0)),
            whole_spec((T, NH)),
            whole_spec((8, 128)),
            whole_spec((128, T)),
        ],
        out_shape=[
            jax.ShapeDtypeStruct((T, width), BF16),
            jax.ShapeDtypeStruct((T, width), BF16),
            jax.ShapeDtypeStruct((8, width), F32),
            jax.ShapeDtypeStruct((8, width), F32),
            jax.ShapeDtypeStruct((PAIRS, 8, 128), F32),
            jax.ShapeDtypeStruct((T, NH), F32),
            jax.ShapeDtypeStruct((8, 128), F32),
            jax.ShapeDtypeStruct((128, T), BF16),
        ],
        scratch_shapes=[
            VM((5, 32, T), F32),
            VM((T, T), F32),
            VM((T, 128), F32),
            VM((3, T, 128), F32),
            VM((8 + T, 128), F32),
            VM((T, STATE), BF16),
            VM((T, STATE), BF16),
            VM((STATE, T), BF16),
            VM((T, T), F32),
            VM((T, T), F32),
            VM((T, T), F32),
            VM((32, T), F32),
            VM((32, T), F32),
            VM((32, T), F32),
            VM((STATE, T), F32),
            VM((STATE, T), F32),
            VM((16 + T, 128), F32),
        ],
        name="mixer_b",
        cost_estimate=pl.CostEstimate(
            flops=3000000000, bytes_accessed=10000000, transcendentals=3000000
        ),
    )(
        conv_input, tail8, gate_input, mix_grad, conv_weight, raw, bias, rate, docc, bin_, cout,
        act_t, g_t, states, skip,
    )


def seq_barrier(me):
    barrier = pltpu.get_barrier_semaphore()

    def greet(k, carry):
        peer = lax.rem(me + k, NSEQ)
        pl.semaphore_signal(barrier, inc=1, device_id={"seq": peer}, device_id_type=MESH)
        return carry

    lax.fori_loop(1, NSEQ, greet, 0)
    pl.semaphore_wait(barrier, NSEQ - 1)


def chain_kernel(loc_ref, thr_ref, out_ref, pay, inbox, outb, landed, s1, r1, s2, r2):
    me = lax.axis_index("seq")
    for e in range(NH):
        pay[e, 0:64, :] = loc_ref[e]
        t = thr_ref[e : e + 1, :]
        hi = t.astype(BF16)
        lo = (t - hi.astype(F32)).astype(BF16)
        pay[e, 64:80, :] = jnp.concatenate(
            [jnp.broadcast_to(hi, (8, 128)), jnp.broadcast_to(lo, (8, 128))], axis=0
        )
    seq_barrier(me)

    def first(peer, src):
        return pltpu.make_async_remote_copy(
            src_ref=pay.at[peer],
            dst_ref=inbox.at[src],
            send_sem=s1.at[peer],
            recv_sem=r1.at[src],
            device_id={"seq": peer},
            device_id_type=MESH,
        )

    def second(peer, src):
        return pltpu.make_async_remote_copy(
            src_ref=outb.at[peer],
            dst_ref=landed.at[src],
            send_sem=s2.at[peer],
            recv_sem=r2.at[src],
            device_id={"seq": peer},
            device_id_type=MESH,
        )

    def send_first(k, carry):
        peer = lax.rem(me + k, NSEQ)

        @pl.when(peer < NH)
        def _():
            first(peer, me).start()

        return carry

    lax.fori_loop(1, NSEQ, send_first, 0)

    @pl.when(me < NH)
    def _():
        inbox[me] = pay[me]

        def wait_first(k, carry):
            src = lax.rem(me + k, NSEQ)
            first(me, src).wait_recv()
            return carry

        lax.fori_loop(1, NSEQ, wait_first, 0)
        lane = lax.broadcasted_iota(jnp.int32, (64, 128), 1)

        def gain(s):
            return inbox[s, 64:65, :].astype(F32) + inbox[s, 72:73, :].astype(F32)

        def down(s, run):
            outb[s] = run.astype(BF16)
            return gain(s) * run + inbox[s, 0:64, :].astype(F32)

        lax.fori_loop(0, NSEQ, down, jnp.zeros((64, 128), F32))

        def up(k, run):
            s = NSEQ - 1 - k
            outb[s] = jnp.where(lane < STATE, outb[s], run.astype(BF16))
            return gain(s) * run + inbox[s, 0:64, :].astype(F32)

        lax.fori_loop(0, NSEQ, up, jnp.zeros((64, 128), F32))

        def send_second(k, carry):
            second(lax.rem(me + k, NSEQ), me).start()
            return carry

        lax.fori_loop(1, NSEQ, send_second, 0)
        landed[me] = outb[me]

    def finish(k, carry):
        peer = lax.rem(me + k, NSEQ)

        @pl.when(peer < NH)
        def _():
            first(peer, me).wait_send()
            second(me, peer).wait_recv()

        return carry

    lax.fori_loop(1, NSEQ, finish, 0)

    @pl.when(me < NH)
    def _():
        def drain(k, carry):
            second(lax.rem(me + k, NSEQ), me).wait_send()
            return carry

        lax.fori_loop(1, NSEQ, drain, 0)

    out_ref[...] = landed[...]


def chain(loc, thr):
    dma = pltpu.SemaphoreType.DMA
    return pl.pallas_call(
        chain_kernel,
        out_shape=jax.ShapeDtypeStruct((NH, 64, 128), BF16),
        scratch_shapes=[
            VM((NH, 80, 128), BF16),
            VM((NSEQ, 80, 128), BF16),
            VM((NSEQ, 64, 128), BF16),
            VM((NH, 64, 128), BF16),
            dma((NSEQ,)),
            dma((NSEQ,)),
            dma((NSEQ,)),
            dma((NSEQ,)),
        ],
        compiler_params=pltpu.CompilerParams(collective_id=1, has_side_effects=True),
        name="state_chain",
        cost_estimate=pl.CostEstimate(flops=20000000, bytes_accessed=1000000, transcendentals=0),
    )(loc, thr)


BLOCKS = PAIRS + 1


def sums_kernel(
    red_ref, scal_ref, coef_ref, spill_ref, last_ref,
    dw_ref, sc_ref, gin_ref, gout_ref, fix_ref,
    src, inbox, tot, cin, spin, s1, r1, s2, r2, s3, r3, s4, r4,
):
    me = lax.axis_index("seq")
    hd = lax.axis_index("head")
    barrier = pltpu.get_barrier_semaphore()

    def greet(k, carry):
        peer = lax.rem(me + k, NSEQ)
        pl.semaphore_signal(barrier, inc=1, device_id={"seq": peer}, device_id_type=MESH)
        return carry

    lax.fori_loop(1, NSEQ, greet, 0)
    for k in range(1, 4):
        pl.semaphore_signal(
            barrier, inc=1, device_id={"head": lax.rem(hd + k, 4)}, device_id_type=MESH
        )
    src[0:PAIRS] = red_ref[...]
    src[PAIRS] = scal_ref[...]
    pl.semaphore_wait(barrier, NSEQ + 2)

    def coef(k, frm):
        return pltpu.make_async_remote_copy(
            src_ref=coef_ref,
            dst_ref=cin.at[frm],
            send_sem=s3.at[k],
            recv_sem=r3.at[frm],
            device_id={"head": lax.rem(hd + k, 4)},
            device_id_type=MESH,
        )

    spill_copy = pltpu.make_async_remote_copy(
        src_ref=spill_ref,
        dst_ref=spin,
        send_sem=s4,
        recv_sem=r4,
        device_id={"seq": lax.rem(me + NSEQ - 1, NSEQ)},
        device_id_type=MESH,
    )

    def first(block, frm):
        return pltpu.make_async_remote_copy(
            src_ref=src.at[block],
            dst_ref=inbox.at[frm],
            send_sem=s1.at[block],
            recv_sem=r1.at[frm],
            device_id={"seq": 2 * block},
            device_id_type=MESH,
        )

    def second(peer, block):
        return pltpu.make_async_remote_copy(
            src_ref=tot.at[block],
            dst_ref=tot.at[block],
            send_sem=s2.at[peer],
            recv_sem=r2.at[block],
            device_id={"seq": peer},
            device_id_type=MESH,
        )

    def send_first(b, carry):
        @pl.when(2 * b != me)
        def _():
            first(b, me).start()

        return carry

    lax.fori_loop(0, BLOCKS, send_first, 0)
    for k in range(1, 4):
        coef(k, hd).start()
    spill_copy.start()
    mine = me // 2
    owner = (me == 2 * mine) & (mine < BLOCKS)

    @pl.when(owner)
    def _():
        inbox[me] = src[mine]

        def wait_first(k, carry):
            first(mine, lax.rem(me + k, NSEQ)).wait_recv()
            return carry

        lax.fori_loop(1, NSEQ, wait_first, 0)
        tot[mine] = jnp.sum(inbox[...], axis=0)

        def send_second(k, carry):
            second(lax.rem(me + k, NSEQ), mine).start()
            return carry

        lax.fori_loop(1, NSEQ, send_second, 0)

    for k in range(1, 4):
        coef(k, lax.rem(hd + k, 4)).wait_recv()
    cin[hd] = coef_ref[...]
    g0 = jnp.transpose(cin[0].astype(F32) + cin[1].astype(F32))
    g1 = jnp.transpose(cin[2].astype(F32) + cin[3].astype(F32))
    gin_ref[...] = jnp.concatenate([g0[:, 0:STATE], g1[:, 0:STATE]], axis=1)
    gout_ref[...] = jnp.concatenate([g0[:, STATE:], g1[:, STATE:]], axis=1)
    spill_copy.wait_recv()
    keep = jnp.where(me == NSEQ - 1, 0.0, 1.0)
    fix_ref[...] = last_ref[...] + keep * spin[...]

    def wait_second(b, carry):
        @pl.when(2 * b != me)
        def _():
            second(me, b).wait_recv()
            first(b, me).wait_send()

        return carry

    lax.fori_loop(0, BLOCKS, wait_second, 0)
    for p in range(PAIRS):
        dw_ref[:, 128 * p : 128 * p + 128] = tot[p, 0:4, :]
    sc_ref[...] = tot[PAIRS]

    @pl.when(owner)
    def _():
        def drain(k, carry):
            second(lax.rem(me + k, NSEQ), mine).wait_send()
            return carry

        lax.fori_loop(1, NSEQ, drain, 0)

    for k in range(1, 4):
        coef(k, hd).wait_send()
    spill_copy.wait_send()


def sums(red, scal, coef, spill, last):
    dma = pltpu.SemaphoreType.DMA
    width = NH * 64
    return pl.pallas_call(
        sums_kernel,
        out_shape=[
            jax.ShapeDtypeStruct((4, width), F32),
            jax.ShapeDtypeStruct((8, 128), F32),
            jax.ShapeDtypeStruct((T, 128), F32),
            jax.ShapeDtypeStruct((T, 128), F32),
            jax.ShapeDtypeStruct((8, width), F32),
        ],
        in_specs=[pl.BlockSpec(memory_space=VM)] * 5,
        out_specs=[pl.BlockSpec(memory_space=VM)] * 5,
        scratch_shapes=[
            VM((BLOCKS, 8, 128), F32),
            VM((NSEQ, 8, 128), F32),
            VM((BLOCKS, 8, 128), F32),
            VM((4, 128, T), BF16),
            VM((8, width), F32),
            dma((BLOCKS,)),
            dma((NSEQ,)),
            dma((NSEQ,)),
            dma((BLOCKS,)),
            dma((4,)),
            dma((4,)),
            dma,
            dma,
        ],
        compiler_params=pltpu.CompilerParams(collective_id=2, has_side_effects=True),
        name="sums",
        cost_estimate=pl.CostEstimate(flops=2000000, bytes_accessed=1000000, transcendentals=0),
    )(red, scal, coef, spill, last)


def local(
    queries, keys, values, attn_grad, doc_ids, conv_input, conv_weight, step_raw, step_bias,
    rate_log, skip_gain, input_coeff, output_coeff, gate_input, mix_grad,
):
    me = lax.axis_index("seq")
    pieces = attn_prep(queries, keys, values, attn_grad)
    halo = [group_shift(pieces[k], k, 1) for k in range(RING)]
    kv = [ring_shift(pieces[k], k) for k in range(RING)]
    qd = [ring_shift(pieces[4 + k], k) for k in range(RING)]
    tail = lax.ppermute(
        conv_input[T - 8 :], "seq", [(s, s + 1) for s in range(NSEQ - 1)]
    ).astype(F32)
    doc_pad = jnp.concatenate([jnp.full((WINDOW,), -1, jnp.int32), doc_ids])
    doc_rows = lax.dynamic_slice_in_dim(doc_pad, me // RING * WINDOW, 2 * WINDOW)
    doc_rows = doc_rows.reshape(8, T).astype(F32)
    ext = lax.dynamic_slice_in_dim(doc_pad, me * T + WINDOW - 3, T + 3)
    doc = ext[3:]
    docc = jnp.stack(
        [doc, doc == ext[2], doc == doc[T - 1]]
        + [doc == ext[3 - k : 3 - k + T] for k in range(1, 4)]
        + [doc, doc]
    ).astype(F32)
    shared = (
        conv_input, tail, gate_input, mix_grad, conv_weight, step_raw, step_bias[None],
        rate_log[None], docc, input_coeff, output_coeff,
    )
    act_t, g_t, loc, thr = phase_a(*shared)
    states = chain(loc.reshape(NH, 64, 128), thr).reshape(NH * 64, 128)
    outs = attn_core(kv, qd, halo, doc_rows)
    own = [ring_shift(outs[k], k) for k in range(RING)]
    back = [group_shift(outs[4 + k], k, -1) for k in range(RING)]
    dconv, dgate, spill, last, red, gstep, scal, coef = phase_b(
        *shared, act_t, g_t, states, skip_gain
    )
    dw, sc, gin, gout, fix = sums(red, scal, coef, spill, last)
    dconv = lax.dynamic_update_slice(dconv, fix.astype(BF16), (T - 8, 0))
    gq, gk, gv = attn_final(own, back)
    return (
        gq, gk, gv, dconv, dgate, gstep, gin, gout, dw, sc[0, :NH], sc[1, :NH], sc[2, :NH]
    )


def solution(mesh):
    both = P("seq", "head")
    return jax.shard_map(
        local,
        mesh=mesh,
        in_specs=(
            both, both, both, both, P(), both, P(None, "head"), both, P("head"), P("head"),
            P("head"), P("seq", None), P("seq", None), both, both,
        ),
        out_specs=(
            both, both, both, both, both, both, P("seq", None), P("seq", None),
            P(None, "head"), P("head"), P("head"), P("head"),
        ),
        check_vma=False,
    )
```

profile of v0, /device:TPU:0, one launch (start us, length us, event | category | flops | bytes accessed | tf_op | source)
XLA Modules:
  0.0 175.1 jit_solution(6512518218345845531)
XLA Ops:
  0.7 0.8 slice.31
  1.4 3.5 %collective-permute-start.17 = (bf16[8,1792]{1,0:T(8,128)(2,1)S(1)}, bf16[8,1792]{1,0:T(8,128)(2,1)S(1)}, u32[]{:S(2)}, u32[]{:S(2)}) collective-permute-start(bf16[8,1792]{1,0:T(8,128)(2,1)S(1)} %slice.31), channel_id=1, source_target_pairs={{0,4},{4,8},{8,12},{12,16},{16,20},{20,24},{24,28},{28,32},{32,36}... | collective-permute-start | bytes 86024 | tf_op jit(solution)/shard_map/ppermute | solution.py:839
  4.9 3.1 %attn_prep.1 = (bf16[2,224,256]{2,1,0:T(8,128)(2,1)}, bf16[2,224,256]{2,1,0:T(8,128)(2,1)}, bf16[2,224,256]{2,1,0:T(8,128)(2,1)}, bf16[2,224,256]{2,1,0:T(8,128)...) custom-call(bf16[256,896]{1,0:T(8,128)(2,1)} %q_ref.1, ...), custom_call_target="tpu_custom_call" | custom-call | flops 4000000 | bytes 4000000 | tf_op jit(solution)/shard_map/attn_prep/pallas_call | solution.py:55
  8.1 1.5 collective-permute-start
  9.6 4.4 %collective-permute-start.1 = (bf16[2,224,256]{2,1,0:T(8,128)(2,1)}, bf16[2,224,256]{2,1,0:T(8,128)(2,1)S(1)}, u32[]{:S(2)}, u32[]{:S(2)}) collective-permute-start(bf16[2,224,256]{2,1,0:T(8,128)(2,1)} %get-tuple-element.50), channel_id=1, source_target_pairs={{0,8},{4,12},{8,0},{12,4},{16,24},{20,28},{24,16},{28,20},{32,40},... | collective-permute-start | bytes 688136 | tf_op jit(solution)/shard_map/ppermute | solution.py:184
  13.9 4.6 %collective-permute-start.6 = (bf16[2,224,256]{2,1,0:T(8,128)(2,1)}, bf16[2,224,256]{2,1,0:T(8,128)(2,1)S(1)}, u32[]{:S(2)}, u32[]{:S(2)}) collective-permute-start(bf16[2,224,256]{2,1,0:T(8,128)(2,1)} %get-tuple-element.48.refs_0_), channel_id=1, source_target_pairs={{0,16},{4,20},{8,24},{12,28},{16,32},{20,36},{24,40},{28,44},{32,4... | collective-permute-start | bytes 688136 | tf_op jit(solution)/shard_map/ppermute | solution.py:195
  18.6 5.5 %collective-permute-start.7 = (bf16[2,224,256]{2,1,0:T(8,128)(2,1)}, bf16[2,224,256]{2,1,0:T(8,128)(2,1)S(1)}, u32[]{:S(2)}, u32[]{:S(2)}) collective-permute-start(bf16[2,224,256]{2,1,0:T(8,128)(2,1)} %get-tuple-element.49), channel_id=1, source_target_pairs={{0,20},{4,24},{8,28},{12,16},{16,36},{20,40},{24,44},{28,32},{32,5... | collective-permute-start | bytes 688136 | tf_op jit(solution)/shard_map/ppermute | solution.py:195
  24.8 3.7 %collective-permute-start.8 = (bf16[2,224,256]{2,1,0:T(8,128)(2,1)}, bf16[2,224,256]{2,1,0:T(8,128)(2,1)S(1)}, u32[]{:S(2)}, u32[]{:S(2)}) collective-permute-start(bf16[2,224,256]{2,1,0:T(8,128)(2,1)} %get-tuple-element.50), channel_id=1, source_target_pairs={{0,24},{4,28},{8,16},{12,20},{16,40},{20,44},{24,32},{28,36},{32,5... | collective-permute-start | bytes 688136 | tf_op jit(solution)/shard_map/ppermute | solution.py:195
  28.5 6.0 %collective-permute-start.9 = (bf16[2,224,256]{2,1,0:T(8,128)(2,1)}, bf16[2,224,256]{2,1,0:T(8,128)(2,1)S(1)}, u32[]{:S(2)}, u32[]{:S(2)}) collective-permute-start(bf16[2,224,256]{2,1,0:T(8,128)(2,1)} %get-tuple-element.51), channel_id=1, source_target_pairs={{0,28},{4,16},{8,20},{12,24},{16,44},{20,32},{24,36},{28,40},{32,6... | collective-permute-start | bytes 688136 | tf_op jit(solution)/shard_map/ppermute | solution.py:195
  34.6 3.4 %collective-permute-start.4 = (bf16[2,224,256]{2,1,0:T(8,128)(2,1)}, bf16[2,224,256]{2,1,0:T(8,128)(2,1)S(1)}, u32[]{:S(2)}, u32[]{:S(2)}) collective-permute-start(bf16[2,224,256]{2,1,0:T(8,128)(2,1)} %get-tuple-element.54), channel_id=1, source_target_pairs={{0,8},{4,12},{8,0},{12,4},{16,24},{20,28},{24,16},{28,20},{32,40},... | collective-permute-start | bytes 688136 | tf_op jit(solution)/shard_map/ppermute | solution.py:184
  38.1 1.2 collective-permute-start.5
  39.3 1.4 compare_convert_fusion
  41.3 0.8 copy.28.raw_ref
  43.3 10.9 %mixer_a.1 = (f32[1792,256]{1,0:T(8,128)}, f32[1792,256]{1,0:T(8,128)}, bf16[1792,128]{1,0:T(8,128)(2,1)}, f32[32,128]{1,0:T(8,128)}) custom-call(bf16[256,1792]{1,0:T(8,128)(2,1)} %conv_ref.3, f32[8,1792]{1,0:T(8,128)} %convert_element_type.21.tail_ref, bf16[256,1792]{1,0:T(8,128)(2,1)} %gate_ref.3, bf16[256,1792]{1,0:T(8,128)(2,1)} %mix_ref.3, ...), custom_call_target="tpu_custom_call" | custom-call | flops 600000000 | bytes 7000000 | tf_op jit(solution)/shard_map/mixer_a/pallas_call | solution.py:280
  54.3 29.8 %state_chain.1 = bf16[28,64,128]{2,1,0:T(8,128)(2,1)} custom-call(bf16[28,64,128]{2,1,0:T(8,128)(2,1)} %bitcast.19, f32[32,128]{1,0:T(8,128)} %get-tuple-element.70.thr_ref), custom_call_target="tpu_custom_call" | custom-call | flops 20000000 | bytes 1000000 | tf_op jit(solution)/shard_map/state_chain/pallas_call | solution.py:643
  85.2 10.4 %attn_core.1 = (bf16[3,224,256]{2,1,0:T(8,128)(2,1)}, bf16[3,224,256]{2,1,0:T(8,128)(2,1)}, bf16[3,224,256]{2,1,0:T(8,128)(2,1)}, bf16[3,224,256]{2,1,0:T(8,128)...) custom-call(bf16[2,224,256]{2,1,0:T(8,128)(2,1)} %get-tuple-element., ...), custom_call_target="tpu_custom_call" | custom-call | flops 3000000000 | bytes 8000000 | tf_op jit(solution)/shard_map/attn_core/pallas_call | solution.py:138
  95.6 1.3 collective-permute-start.13
  96.9 1.3 collective-permute-start.14
  98.3 16.9 %mixer_b.1 = (bf16[256,1792]{1,0:T(8,128)(2,1)}, bf16[256,1792]{1,0:T(8,128)(2,1)}, f32[8,1792]{1,0:T(8,128)}, f32[8,1792]{1,0:T(8,128)}, f32[14,8,128]{2,1,0:T(...) custom-call(bf16[256,1792]{1,0:T(8,128)(2,1)} %conv_ref.3, ...), custom_call_target="tpu_custom_call" | custom-call | flops 3000000000 | bytes 10000000 | tf_op jit(solution)/shard_map/mixer_b/pallas_call | solution.py:459
  115.2 27.0 %sums.1 = (f32[4,1792]{1,0:T(4,128)}, f32[8,128]{1,0:T(8,128)}, f32[256,128]{1,0:T(8,128)}, f32[256,128]{1,0:T(8,128)}, f32[8,1792]{1,0:T(8,128)}) custom-call(f32[14,8,128]{2,1,0:T(8,128)} %get-tuple-element.72.red_ref, f32[8,128]{1,0:T(8,128)} %get-tuple-element.73.scal_ref, bf16[128,256]{1,0:T(8,128)(2,1)} %get-tuple-element.74.coef_ref, ...), custom_call_target="tpu_custom_call" | custom-call | flops 2000000 | bytes 1000000 | tf_op jit(solution)/shard_map/sums/pallas_call | solution.py:798
  142.3 2.3 %collective-permute-start.11 = (bf16[3,224,256]{2,1,0:T(8,128)(2,1)S(1)}, bf16[3,224,256]{2,1,0:T(8,128)(2,1)S(1)}, u32[]{:S(2)}, u32[]{:S(2)}) collective-permute-start(bf16[3,224,256]{2,1,0:T(8,128)(2,1)S(1)} %copy-done.13), channel_id=1, source_target_pairs={{0,8},{4,12},{8,0},{12,4},{16,24},{20,28},{24,16},{28,20},{32,40},... | collective-permute-start | bytes 1032200 | tf_op jit(solution)/shard_map/ppermute | solution.py:184
  144.7 1.9 %collective-permute-start.12 = (bf16[3,224,256]{2,1,0:T(8,128)(2,1)S(1)}, bf16[3,224,256]{2,1,0:T(8,128)(2,1)S(1)}, u32[]{:S(2)}, u32[]{:S(2)}) collective-permute-start(bf16[3,224,256]{2,1,0:T(8,128)(2,1)S(1)} %copy-done.12), channel_id=1, source_target_pairs={{0,12},{4,0},{8,4},{12,8},{16,28},{20,16},{24,20},{28,24},{32,44},... | collective-permute-start | bytes 1032200 | tf_op jit(solution)/shard_map/ppermute | solution.py:184
  146.5 1.3 collective-permute-start.15
  147.9 1.3 collective-permute-start.16
  149.2 1.4 convert_dynamic-update-slice_fusion
  150.6 1.6 copy.29
  152.2 1.3 slice_bitcast_fusion
  153.5 11.4 %collective-permute-done.15.refs_6_ = bf16[2,224,256]{2,1,0:T(8,128)(2,1)S(1)} collective-permute-done((bf16[2,224,256]{2,1,0:T(8,128)(2,1)}, bf16[2,224,256]{2,1,0:T(8,128)(2,1)S(1)}, u32[]{:S(2)}, u32[]{:S(2)}) %collective-permute-start.15) | collective-permute-done | bytes 229408 | tf_op jit(solution)/shard_map/ppermute | solution.py:195
  164.9 4.1 %collective-permute-done.16.refs_7_ = bf16[2,224,256]{2,1,0:T(8,128)(2,1)S(1)} collective-permute-done((bf16[2,224,256]{2,1,0:T(8,128)(2,1)S(1)}, bf16[2,224,256]{2,1,0:T(8,128)(2,1)S(1)}, u32[]{:S(2)}, u32[]{:S(2)}) %collective-permute-start.16) | collective-permute-done | bytes 229408 | tf_op jit(solution)/shard_map/ppermute | solution.py:195
  170.1 3.1 %attn_final.1 = (bf16[256,896]{1,0:T(8,128)(2,1)}, bf16[256,896]{1,0:T(8,128)(2,1)}, bf16[256,896]{1,0:T(8,128)(2,1)}) custom-call(bf16[3,224,256]{2,1,0:T(8,128)(2,1)} %get-tuple-element.56.refs_0_, bf16[3,224,256]{2,1,0:T(8,128)(2,1)} %copy-done, bf16[3,224,256]{2,1,0:T(8,128)(2,1)} %copy-done.1, bf16[3,224,256]{2,1,0:T(8,128)(2,1)} %copy-done.2, ...), custom_call_target="tpu_custom_call" | custom-call | flops 4000000 | bytes 4000000 | tf_op jit(solution)/shard_map/attn_final/pallas_call | solution.py:172
  173.2 0.7 copy.34
  173.8 0.7 copy.35
  (80 shorter events, 5.4 us)
Async XLA Ops:
  0.6 23.5 %copy-start.9 = (s32[8192]{0:T(1024)S(1)}, s32[8192]{0:T(1024)}, u32[]{:S(2)}) copy-start(s32[8192]{0:T(1024)} %param.19) | copy-start | bytes 98308
  0.7 40.7 %copy-start.10 = (f32[256,28]{0,1:T(8,128)S(1)}, f32[256,28]{0,1:T(8,128)}, u32[]{:S(2)}) copy-start(f32[256,28]{0,1:T(8,128)} %param.22) | copy-start | bytes 86020
  1.4 17.1 %collective-permute-start.17 = (bf16[8,1792]{1,0:T(8,128)(2,1)S(1)}, bf16[8,1792]{1,0:T(8,128)(2,1)S(1)}, u32[]{:S(2)}, u32[]{:S(2)}) collective-permute-start(bf16[8,1792]{1,0:T(8,128)(2,1)S(1)} %slice.31), channel_id=1, source_target_pairs={{0,4},{4,8},{8,12},{12,16},{16,20},{20,24},{24,28},{28,32},{32,36}... | collective-permute-start | bytes 86024 | tf_op jit(solution)/shard_map/ppermute | solution.py:839
  8.1 16.7 %collective-permute-start = (bf16[2,224,256]{2,1,0:T(8,128)(2,1)}, bf16[2,224,256]{2,1,0:T(8,128)(2,1)S(1)}, u32[]{:S(2)}, u32[]{:S(2)}) collective-permute-start(bf16[2,224,256]{2,1,0:T(8,128)(2,1)} %get-tuple-element.49), channel_id=1, source_target_pairs={{0,4},{4,8},{8,12},{12,0},{16,20},{20,24},{24,28},{28,16},{32,36},... | collective-permute-start | bytes 688136 | tf_op jit(solution)/shard_map/ppermute | solution.py:184
  9.6 18.9 %collective-permute-start.1 = (bf16[2,224,256]{2,1,0:T(8,128)(2,1)}, bf16[2,224,256]{2,1,0:T(8,128)(2,1)S(1)}, u32[]{:S(2)}, u32[]{:S(2)}) collective-permute-start(bf16[2,224,256]{2,1,0:T(8,128)(2,1)} %get-tuple-element.50), channel_id=1, source_target_pairs={{0,8},{4,12},{8,0},{12,4},{16,24},{20,28},{24,16},{28,20},{32,40},... | collective-permute-start | bytes 688136 | tf_op jit(solution)/shard_map/ppermute | solution.py:184
  13.9 20.6 %collective-permute-start.2 = (bf16[2,224,256]{2,1,0:T(8,128)(2,1)}, bf16[2,224,256]{2,1,0:T(8,128)(2,1)S(1)}, u32[]{:S(2)}, u32[]{:S(2)}) collective-permute-start(bf16[2,224,256]{2,1,0:T(8,128)(2,1)} %get-tuple-element.51), channel_id=1, source_target_pairs={{0,12},{4,0},{8,4},{12,8},{16,28},{20,16},{24,20},{28,24},{32,44},... | collective-permute-start | bytes 688136 | tf_op jit(solution)/shard_map/ppermute | solution.py:184
  13.9 20.7 %collective-permute-start.6 = (bf16[2,224,256]{2,1,0:T(8,128)(2,1)}, bf16[2,224,256]{2,1,0:T(8,128)(2,1)S(1)}, u32[]{:S(2)}, u32[]{:S(2)}) collective-permute-start(bf16[2,224,256]{2,1,0:T(8,128)(2,1)} %get-tuple-element.48.refs_0_), channel_id=1, source_target_pairs={{0,16},{4,20},{8,24},{12,28},{16,32},{20,36},{24,40},{28,44},{32,4... | collective-permute-start | bytes 688136 | tf_op jit(solution)/shard_map/ppermute | solution.py:195
  18.6 19.5 %collective-permute-start.7 = (bf16[2,224,256]{2,1,0:T(8,128)(2,1)}, bf16[2,224,256]{2,1,0:T(8,128)(2,1)S(1)}, u32[]{:S(2)}, u32[]{:S(2)}) collective-permute-start(bf16[2,224,256]{2,1,0:T(8,128)(2,1)} %get-tuple-element.49), channel_id=1, source_target_pairs={{0,20},{4,24},{8,28},{12,16},{16,36},{20,40},{24,44},{28,32},{32,5... | collective-permute-start | bytes 688136 | tf_op jit(solution)/shard_map/ppermute | solution.py:195
  24.8 59.3 %copy-start.15 = (bf16[2,224,256]{2,1,0:T(8,128)(2,1)}, bf16[2,224,256]{2,1,0:T(8,128)(2,1)S(1)}, u32[]{:S(2)}) copy-start(bf16[2,224,256]{2,1,0:T(8,128)(2,1)S(1)} %collective-permute-done.refs_1_) | copy-start | bytes 688132
  24.8 59.4 %collective-permute-start.8 = (bf16[2,224,256]{2,1,0:T(8,128)(2,1)}, bf16[2,224,256]{2,1,0:T(8,128)(2,1)S(1)}, u32[]{:S(2)}, u32[]{:S(2)}) collective-permute-start(bf16[2,224,256]{2,1,0:T(8,128)(2,1)} %get-tuple-element.50), channel_id=1, source_target_pairs={{0,24},{4,28},{8,16},{12,20},{16,40},{20,44},{24,32},{28,36},{32,5... | collective-permute-start | bytes 688136 | tf_op jit(solution)/shard_map/ppermute | solution.py:195
  28.5 55.6 %copy-start.16 = (bf16[2,224,256]{2,1,0:T(8,128)(2,1)}, bf16[2,224,256]{2,1,0:T(8,128)(2,1)S(1)}, u32[]{:S(2)}) copy-start(bf16[2,224,256]{2,1,0:T(8,128)(2,1)S(1)} %collective-permute-done.1.refs_2_) | copy-start | bytes 688132
  28.5 55.7 %collective-permute-start.9 = (bf16[2,224,256]{2,1,0:T(8,128)(2,1)}, bf16[2,224,256]{2,1,0:T(8,128)(2,1)S(1)}, u32[]{:S(2)}, u32[]{:S(2)}) collective-permute-start(bf16[2,224,256]{2,1,0:T(8,128)(2,1)} %get-tuple-element.51), channel_id=1, source_target_pairs={{0,28},{4,16},{8,20},{12,24},{16,44},{20,32},{24,36},{28,40},{32,6... | collective-permute-start | bytes 688136 | tf_op jit(solution)/shard_map/ppermute | solution.py:195
  34.5 49.6 %copy-start.17 = (bf16[2,224,256]{2,1,0:T(8,128)(2,1)}, bf16[2,224,256]{2,1,0:T(8,128)(2,1)S(1)}, u32[]{:S(2)}) copy-start(bf16[2,224,256]{2,1,0:T(8,128)(2,1)S(1)} %collective-permute-done.2.refs_3_) | copy-start | bytes 688132
  34.5 49.7 %collective-permute-start.3 = (bf16[2,224,256]{2,1,0:T(8,128)(2,1)}, bf16[2,224,256]{2,1,0:T(8,128)(2,1)S(1)}, u32[]{:S(2)}, u32[]{:S(2)}) collective-permute-start(bf16[2,224,256]{2,1,0:T(8,128)(2,1)} %get-tuple-element.53), channel_id=1, source_target_pairs={{0,4},{4,8},{8,12},{12,0},{16,20},{20,24},{24,28},{28,16},{32,36},... | collective-permute-start | bytes 688136 | tf_op jit(solution)/shard_map/ppermute | solution.py:184
  34.6 49.5 %copy-start.18 = (bf16[2,224,256]{2,1,0:T(8,128)(2,1)}, bf16[2,224,256]{2,1,0:T(8,128)(2,1)S(1)}, u32[]{:S(2)}) copy-start(bf16[2,224,256]{2,1,0:T(8,128)(2,1)S(1)} %collective-permute-done.6.refs_8_) | copy-start | bytes 688132
  34.6 49.6 %collective-permute-start.4 = (bf16[2,224,256]{2,1,0:T(8,128)(2,1)}, bf16[2,224,256]{2,1,0:T(8,128)(2,1)S(1)}, u32[]{:S(2)}, u32[]{:S(2)}) collective-permute-start(bf16[2,224,256]{2,1,0:T(8,128)(2,1)} %get-tuple-element.54), channel_id=1, source_target_pairs={{0,8},{4,12},{8,0},{12,4},{16,24},{20,28},{24,16},{28,20},{32,40},... | collective-permute-start | bytes 688136 | tf_op jit(solution)/shard_map/ppermute | solution.py:184
  38.1 46.1 %copy-start.19 = (bf16[2,224,256]{2,1,0:T(8,128)(2,1)}, bf16[2,224,256]{2,1,0:T(8,128)(2,1)S(1)}, u32[]{:S(2)}) copy-start(bf16[2,224,256]{2,1,0:T(8,128)(2,1)S(1)} %collective-permute-done.7.refs_9_) | copy-start | bytes 688132
  38.1 46.2 %collective-permute-start.5 = (bf16[2,224,256]{2,1,0:T(8,128)(2,1)}, bf16[2,224,256]{2,1,0:T(8,128)(2,1)S(1)}, u32[]{:S(2)}, u32[]{:S(2)}) collective-permute-start(bf16[2,224,256]{2,1,0:T(8,128)(2,1)} %get-tuple-element.55), channel_id=1, source_target_pairs={{0,12},{4,0},{8,4},{12,8},{16,28},{20,16},{24,20},{28,24},{32,44},... | collective-permute-start | bytes 688136 | tf_op jit(solution)/shard_map/ppermute | solution.py:184
  95.6 50.9 %collective-permute-start.13 = (bf16[2,224,256]{2,1,0:T(8,128)(2,1)}, bf16[2,224,256]{2,1,0:T(8,128)(2,1)S(1)}, u32[]{:S(2)}, u32[]{:S(2)}) collective-permute-start(bf16[2,224,256]{2,1,0:T(8,128)(2,1)} %get-tuple-element.60), channel_id=1, source_target_pairs={{16,0},{20,4},{24,8},{28,12},{32,16},{36,20},{40,24},{44,28},{48,3... | collective-permute-start | bytes 688136 | tf_op jit(solution)/shard_map/ppermute | solution.py:195
  96.9 50.9 %collective-permute-start.14 = (bf16[2,224,256]{2,1,0:T(8,128)(2,1)}, bf16[2,224,256]{2,1,0:T(8,128)(2,1)S(1)}, u32[]{:S(2)}, u32[]{:S(2)}) collective-permute-start(bf16[2,224,256]{2,1,0:T(8,128)(2,1)} %get-tuple-element.61), channel_id=1, source_target_pairs={{16,4},{20,8},{24,12},{28,0},{32,20},{36,24},{40,28},{44,16},{48,3... | collective-permute-start | bytes 688136 | tf_op jit(solution)/shard_map/ppermute | solution.py:195
  98.2 44.0 %copy-start.14 = (bf16[3,224,256]{2,1,0:T(8,128)(2,1)S(1)}, bf16[3,224,256]{2,1,0:T(8,128)(2,1)}, u32[]{:S(2)}) copy-start(bf16[3,224,256]{2,1,0:T(8,128)(2,1)} %get-tuple-element.57) | copy-start | bytes 1032196
  98.2 44.1 %copy-start.13 = (bf16[3,224,256]{2,1,0:T(8,128)(2,1)S(1)}, bf16[3,224,256]{2,1,0:T(8,128)(2,1)}, u32[]{:S(2)}) copy-start(bf16[3,224,256]{2,1,0:T(8,128)(2,1)} %get-tuple-element.58) | copy-start | bytes 1032196
  98.3 46.4 %copy-start.12 = (bf16[3,224,256]{2,1,0:T(8,128)(2,1)S(1)}, bf16[3,224,256]{2,1,0:T(8,128)(2,1)}, u32[]{:S(2)}) copy-start(bf16[3,224,256]{2,1,0:T(8,128)(2,1)} %get-tuple-element.59) | copy-start | bytes 1032196
  98.3 49.6 %copy-start.25 = (bf16[2,224,256]{2,1,0:T(8,128)(2,1)S(1)}, bf16[2,224,256]{2,1,0:T(8,128)(2,1)}, u32[]{:S(2)}) copy-start(bf16[2,224,256]{2,1,0:T(8,128)(2,1)} %get-tuple-element.63) | copy-start | bytes 688132
  142.2 31.0 %copy-start.8 = (f32[256,128]{1,0:T(8,128)S(1)}, f32[256,128]{1,0:T(8,128)}, u32[]{:S(2)}) copy-start(f32[256,128]{1,0:T(8,128)} %get-tuple-element.124) | copy-start | bytes 393220
  142.2 31.6 %copy-start.7 = (f32[256,128]{1,0:T(8,128)S(1)}, f32[256,128]{1,0:T(8,128)}, u32[]{:S(2)}) copy-start(f32[256,128]{1,0:T(8,128)} %get-tuple-element.125) | copy-start | bytes 393220
  142.2 32.3 %copy-start.11 = (f32[4,1792]{1,0:T(4,128)S(1)}, f32[4,1792]{1,0:T(4,128)}, u32[]{:S(2)}) copy-start(f32[4,1792]{1,0:T(4,128)} %get-tuple-element.126) | copy-start | bytes 86020
  142.2 26.8 %collective-permute-start.10 = (bf16[3,224,256]{2,1,0:T(8,128)(2,1)S(1)}, bf16[3,224,256]{2,1,0:T(8,128)(2,1)S(1)}, u32[]{:S(2)}, u32[]{:S(2)}) collective-permute-start(bf16[3,224,256]{2,1,0:T(8,128)(2,1)S(1)} %copy-done.14), channel_id=1, source_target_pairs={{0,4},{4,8},{8,12},{12,0},{16,20},{20,24},{24,28},{28,16},{32,36},... | collective-permute-start | bytes 1032200 | tf_op jit(solution)/shard_map/ppermute | solution.py:184
  142.3 26.7 %collective-permute-start.11 = (bf16[3,224,256]{2,1,0:T(8,128)(2,1)S(1)}, bf16[3,224,256]{2,1,0:T(8,128)(2,1)S(1)}, u32[]{:S(2)}, u32[]{:S(2)}) collective-permute-start(bf16[3,224,256]{2,1,0:T(8,128)(2,1)S(1)} %copy-done.13), channel_id=1, source_target_pairs={{0,8},{4,12},{8,0},{12,4},{16,24},{20,28},{24,16},{28,20},{32,40},... | collective-permute-start | bytes 1032200 | tf_op jit(solution)/shard_map/ppermute | solution.py:184
  144.7 24.3 %collective-permute-start.12 = (bf16[3,224,256]{2,1,0:T(8,128)(2,1)S(1)}, bf16[3,224,256]{2,1,0:T(8,128)(2,1)S(1)}, u32[]{:S(2)}, u32[]{:S(2)}) collective-permute-start(bf16[3,224,256]{2,1,0:T(8,128)(2,1)S(1)} %copy-done.12), channel_id=1, source_target_pairs={{0,12},{4,0},{8,4},{12,8},{16,28},{20,16},{24,20},{28,24},{32,44},... | collective-permute-start | bytes 1032200 | tf_op jit(solution)/shard_map/ppermute | solution.py:184
  146.5 18.4 %collective-permute-start.15 = (bf16[2,224,256]{2,1,0:T(8,128)(2,1)}, bf16[2,224,256]{2,1,0:T(8,128)(2,1)S(1)}, u32[]{:S(2)}, u32[]{:S(2)}) collective-permute-start(bf16[2,224,256]{2,1,0:T(8,128)(2,1)} %get-tuple-element.62), channel_id=1, source_target_pairs={{16,8},{20,12},{24,0},{28,4},{32,24},{36,28},{40,16},{44,20},{48,4... | collective-permute-start | bytes 688136 | tf_op jit(solution)/shard_map/ppermute | solution.py:195
  147.9 21.1 %collective-permute-start.16 = (bf16[2,224,256]{2,1,0:T(8,128)(2,1)S(1)}, bf16[2,224,256]{2,1,0:T(8,128)(2,1)S(1)}, u32[]{:S(2)}, u32[]{:S(2)}) collective-permute-start(bf16[2,224,256]{2,1,0:T(8,128)(2,1)S(1)} %copy-done.25), channel_id=1, source_target_pairs={{16,12},{20,0},{24,4},{28,8},{32,28},{36,16},{40,20},{44,24},{48,4... | collective-permute-start | bytes 688136 | tf_op jit(solution)/shard_map/ppermute | solution.py:195
  (12 other events, 55.3 us)
where the time goes:
time: 177 us; the launch traced here: 175 us
  Pallas kernels  101 us (57%)
  starting transfers between devices  43.3 us (24%)
  waiting for transfers between devices  15.5 us (9%)
  local copies, waits for them, and re-layouts  9.76 us (6%)
  other arithmetic  4.03 us (2%)
    pallas_call x1, Pallas kernels, chain(): pl.pallas_call(chain_kernel, out_shape=jax.ShapeDtypeStruct((NH, 64, 128)...  29.8 us
    pallas_call x1, Pallas kernels, sums(): pl.pallas_call(sums_kernel, out_shape=[jax.ShapeDtypeStruct((4, width), F...  27 us
    ppermute x8, starting transfers between devices, group_shift(): return lax.ppermute(value, 'seq', pairs)  25 us
    pallas_call x1, Pallas kernels, phase_b(): pl.pallas_call(phase_b_kernel, grid=(PAIRS,), in_specs=[tok, row8, tok, t...  16.9 us
    ppermute x8, waiting for transfers between devices, group_shift(): return lax.ppermute(value, 'seq', pairs)  15.5 us
    ppermute x9, starting transfers between devices, ring_shift(): lax.ppermute(value, 'seq', [(s, s // RING * RING + (s + k) % RING) for s...  14.9 us
    pallas_call x1, Pallas kernels, phase_a(): pl.pallas_call(phase_a_kernel, grid=(PAIRS,), in_specs=[tok, pl.BlockSpec...  10.9 us
    pallas_call x1, Pallas kernels, attn_core(): pl.pallas_call(attn_kernel, out_shape=[jax.ShapeDtypeStruct((3, HEAD_DIM,...  10.4 us
  transfers between devices with their start and end apart: 18, of which 2 were waited for; matrix products, arithmetic and copies ran while one was open for 5% of the time, Pallas kernels for 50%

commit v1 on v0

v1 whole, which is shorter than its diff:
```python
import jax
import jax.numpy as jnp
from jax import lax
from jax.experimental import pallas as pl
from jax.experimental.pallas import tpu as pltpu
from jax.sharding import PartitionSpec as P

HEAD_DIM = 224
WINDOW = 1024
SSM_HEADS = 112
STATE = 64
GROUPS = 2
T = 256
NH = 28
PAIRS = 14
NSEQ = 32
RING = 4
NEG = -1e30
F32 = jnp.float32
BF16 = jnp.bfloat16
MESH = pl.DeviceIdType.MESH
VM = pltpu.VMEM
SCALE = HEAD_DIM ** (-0.5)
HI = lax.Precision.HIGHEST


def dot(a, b, ca, cb, precision=None):
    return lax.dot_general(
        a, b, (((ca,), (cb,)), ((), ())), preferred_element_type=F32, precision=precision
    )


def sigmoid(v):
    return 1.0 / (1.0 + jnp.exp(-v))


def col_of(row, rows):
    return jnp.transpose(jnp.broadcast_to(row, (rows, row.shape[1])))


def attn_kernel(*refs):
    kv, qd, halo, doc_ref, own, back, akv, aqd, dka, dva, doq = refs
    x = lax.rem(lax.axis_index("seq"), RING)
    for k in range(RING):
        c = lax.rem(x - k + RING, RING)
        akv[RING + c] = kv[k][...]
        akv[c] = halo[k][...]
        aqd[c] = qd[k][...]
    dka[...] = jnp.zeros_like(dka)
    dva[...] = jnp.zeros_like(dva)
    row_i = lax.broadcasted_iota(jnp.int32, (T, T), 0)
    col_j = lax.broadcasted_iota(jnp.int32, (T, T), 1)

    def chunk(c, carry):
        qt = aqd[c, 0]
        gt = aqd[c, 1]
        q = jnp.transpose(qt.astype(F32)).astype(BF16)
        g = jnp.transpose(gt.astype(F32)).astype(BF16)
        dq_col = col_of(doc_ref[pl.ds(RING + c, 1), :], 128)
        dq_col = jnp.concatenate([dq_col, dq_col], axis=1)
        scores, masks = [], []
        row_max = None
        for b in range(RING + 1):
            s = dot(q, akv[c + b, 0], 1, 0) * SCALE
            ok = dq_col == doc_ref[pl.ds(c + b, 1), :]
            if b == 0:
                ok = ok & (col_j > row_i)
            if b == RING:
                ok = ok & (col_j <= row_i)
            s = jnp.where(ok, s, NEG)
            scores.append(s)
            masks.append(ok)
            m = jnp.max(s, axis=1, keepdims=True)
            row_max = m if row_max is None else jnp.maximum(row_max, m)
        row_sum = None
        for b in range(RING + 1):
            e = jnp.where(masks[b], jnp.exp(scores[b] - row_max), 0.0)
            scores[b] = e
            r = jnp.sum(e, axis=1, keepdims=True)
            row_sum = r if row_sum is None else row_sum + r
        inv = 1.0 / jnp.maximum(row_sum, 1.0)
        dprobs = []
        delta = None
        for b in range(RING + 1):
            p = scores[b] * inv
            scores[b] = p
            half = p.astype(BF16)
            dp = dot(g, akv[c + b, 1], 1, 0)
            dprobs.append(dp)
            r = jnp.sum(half.astype(F32) * dp, axis=1, keepdims=True)
            delta = r if delta is None else delta + r
            dva[c + b] = dva[c + b] + dot(gt, half, 1, 0)
        dqt = None
        for b in range(RING + 1):
            ds = (scores[b] * (dprobs[b] - delta)).astype(BF16)
            r = dot(akv[c + b, 0], ds, 1, 1)
            dqt = r if dqt is None else dqt + r
            dka[c + b] = dka[c + b] + dot(qt, ds, 1, 0)
        doq[c] = dqt
        return carry

    lax.fori_loop(0, RING, chunk, 0)
    for k in range(RING):
        c = lax.rem(x + k, RING)
        own[k, 0] = (doq[c] * SCALE).astype(BF16)
        own[k, 1] = (dka[RING + c] * SCALE).astype(BF16)
        own[k, 2] = dva[RING + c].astype(BF16)
        back[k, 0] = (dka[c] * SCALE).astype(BF16)
        back[k, 1] = dva[c].astype(BF16)


def attn_core(kv, qd, halo, doc_rows):
    return pl.pallas_call(
        attn_kernel,
        out_shape=[
            jax.ShapeDtypeStruct((RING, 3, HEAD_DIM, T), BF16),
            jax.ShapeDtypeStruct((RING, 2, HEAD_DIM, T), BF16),
        ],
        scratch_shapes=[
            VM((2 * RING, 2, HEAD_DIM, T), BF16),
            VM((RING, 2, HEAD_DIM, T), BF16),
            VM((2 * RING, HEAD_DIM, T), F32),
            VM((2 * RING, HEAD_DIM, T), F32),
            VM((RING, HEAD_DIM, T), F32),
        ],
        name="attn_core",
        cost_estimate=pl.CostEstimate(
            flops=3000000000, bytes_accessed=8000000, transcendentals=1400000
        ),
    )(kv, qd, halo, doc_rows)


def mixer_setup(raw_ref, bias_ref, rate_ref, docc_ref, rows, tri, scr, mk):
    scr[...] = jnp.zeros_like(scr)
    step = jnp.log(1.0 + jnp.exp(raw_ref[...] + bias_ref[...]))
    scr[:, 0:NH] = step
    rows[0] = jnp.transpose(scr[...])[0:32]
    scr[:, 0:NH] = -step * jnp.exp(rate_ref[...])
    ld = jnp.transpose(scr[...])[0:32]
    rows[1] = ld
    i = lax.broadcasted_iota(jnp.int32, (T, T), 0)
    j = lax.broadcasted_iota(jnp.int32, (T, T), 1)
    tri[...] = jnp.where(i <= j, 1.0, 0.0)
    cum = dot(ld, tri[...], 1, 0, HI)
    rows[2] = cum
    rows[3] = jnp.where(docc_ref[1:2, :] > 0.0, jnp.exp(cum), 0.0)
    rows[4] = jnp.where(
        docc_ref[2:3, :] > 0.0, jnp.exp(jnp.minimum(cum[:, T - 1 : T] - cum, 0.0)), 0.0
    )
    for k in range(3):
        mk[k] = col_of(docc_ref[3 + k : 4 + k, :], 128)


def pair_rows(rows, which, pair):
    a = rows[which, pl.ds(2 * pair, 1), :]
    b = rows[which, pl.ds(2 * pair + 1, 1), :]
    return jnp.concatenate(
        [jnp.broadcast_to(a, (64, T)), jnp.broadcast_to(b, (64, T))], axis=0
    )


def group_cols(ref, group):
    v = ref[...].astype(F32)
    return jnp.where(group == 0, v[:, 0:STATE], v[:, STATE:])


def conv_forward(x, tail, w_ref, mk, xs):
    xs[0:8, :] = tail
    xs[8 : 8 + T, :] = x
    pre = w_ref[0:1, :] * x
    for k in range(1, 4):
        pre = pre + w_ref[k : k + 1, :] * (mk[k - 1] * xs[8 - k : 8 - k + T, :])
    return pre


def seq_copy(src, dst, send, recv, peer):
    return pltpu.make_async_remote_copy(
        src_ref=src,
        dst_ref=dst,
        send_sem=send,
        recv_sem=recv,
        device_id={"seq": peer},
        device_id_type=MESH,
    )


def greet_seq(barrier, me):
    def greet(k, carry):
        peer = lax.rem(me + k, NSEQ)
        pl.semaphore_signal(barrier, inc=1, device_id={"seq": peer}, device_id_type=MESH)
        return carry

    lax.fori_loop(1, NSEQ, greet, 0)


def tail_rows(ref, pair):
    lanes = pl.ds(pl.multiple_of(pair * 128, 128), 128)
    return ref[:, lanes].astype(F32)[8:16]


def front_kernel(
    conv_ref, gate_ref, mix_ref, w_ref, raw_ref, bias_ref, rate_ref, docc_ref, bin_ref, cout_ref,
    q_ref, k_ref, v_ref, do_ref, edge_ref,
    act_out, g_out, st_out, tail_out, kv_out, qd_out, halo_out,
    rows, tri, scr, mk, xs, bg, cg, kvp, qdp, tscr, tail_in, pay, inbox, outb, landed,
    hs, hr, ks, kr, qs, qr, ts, tr, ls, s1, r1, s2, r2,
):
    pair = pl.program_id(0)
    me = lax.axis_index("seq")
    x_me = lax.rem(me, RING)
    base = me - x_me
    fwd = lax.rem(base + RING, NSEQ)

    def halo_copy(k):
        return seq_copy(
            kvp.at[k], halo_out.at[k], hs.at[k], hr.at[k], fwd + lax.rem(x_me + k, RING)
        )

    def own_copy(k, src, dst, send, recv):
        return seq_copy(
            src.at[k], dst.at[k], send.at[k], recv.at[k], base + lax.rem(x_me + k, RING)
        )

    def stay(src, dst, i):
        return pltpu.make_async_copy(src.at[0], dst.at[0], ls.at[i])

    tail_copy = seq_copy(edge_ref, tail_in, ts, tr, lax.rem(me + 1, NSEQ))

    @pl.when(pair == 0)
    def _():
        barrier = pltpu.get_barrier_semaphore()
        greet_seq(barrier, me)
        for slot, (src, dest) in enumerate(((k_ref, kvp), (v_ref, kvp), (q_ref, qdp), (do_ref, qdp))):
            tscr[...] = jnp.transpose(src[...].astype(F32)).astype(BF16)
            for k in range(RING):
                h = lax.rem(x_me + k, RING)
                dest[k, slot % 2] = tscr[pl.ds(pl.multiple_of(h * HEAD_DIM, 32), HEAD_DIM), :]
        pl.semaphore_wait(barrier, NSEQ - 1)
        tail_copy.start()
        for k in range(RING):
            halo_copy(k).start()
            if k:
                own_copy(k, kvp, kv_out, ks, kr).start()
        stay(kvp, kv_out, 0).start()
        stay(qdp, qd_out, 1).start()
        mixer_setup(raw_ref, bias_ref, rate_ref, docc_ref, rows, tri, scr, mk)
        group = lax.axis_index("head") // 2
        bg[...] = group_cols(bin_ref, group).astype(BF16)
        cg[...] = group_cols(cout_ref, group).astype(BF16)
        thr = rows[3][:, T - 1 : T]
        for e in range(NH):
            t = jnp.broadcast_to(thr[e : e + 1, :], (8, 128))
            hi = t.astype(BF16).astype(F32)
            pay[e, 64:80, :] = jnp.concatenate([hi, t - hi], axis=0).astype(BF16)
        tail_copy.wait_recv()
        tail_out[...] = tail_in[...]

    x = conv_ref[...].astype(F32)
    pre = conv_forward(x, tail_rows(tail_in, pair), w_ref, mk, xs)
    act = pre * sigmoid(pre)
    gate = gate_ref[...].astype(F32)
    g = mix_ref[...].astype(F32) * (gate * sigmoid(gate))
    act_t = jnp.transpose(act)
    g_t = jnp.transpose(g)
    act_out[...] = act_t
    g_out[...] = g_t
    st = act_t * (pair_rows(rows, 0, pair) * pair_rows(rows, 4, pair))
    ge = g_t * pair_rows(rows, 3, pair)
    both = jnp.concatenate(
        [dot(st.astype(BF16), bg[...], 1, 0), dot(ge.astype(BF16), cg[...], 1, 0)], axis=1
    ).astype(BF16)
    pay[2 * pair, 0:64, :] = both[0:64]
    pay[2 * pair + 1, 0:64, :] = both[64:128]

    def first(peer, frm):
        return seq_copy(pay.at[peer], inbox.at[frm], s1.at[peer], r1.at[frm], peer)

    def second(peer, frm):
        return seq_copy(outb.at[peer], landed.at[frm], s2.at[peer], r2.at[frm], peer)

    @pl.when(pair == PAIRS - 1)
    def _():
        def send_first(k, carry):
            peer = lax.rem(me + k, NSEQ)

            @pl.when(peer < NH)
            def _():
                first(peer, me).start()

            return carry

        lax.fori_loop(1, NSEQ, send_first, 0)
        for k in range(1, RING):
            own_copy(k, qdp, qd_out, qs, qr).start()

        @pl.when(me < NH)
        def _():
            inbox[me] = pay[me]

            def wait_first(k, carry):
                first(me, lax.rem(me + k, NSEQ)).wait_recv()
                return carry

            lax.fori_loop(1, NSEQ, wait_first, 0)
            lane = lax.broadcasted_iota(jnp.int32, (64, 128), 1)

            def gain(s):
                tail = inbox[s, 64:80, :].astype(F32)
                return tail[0:1] + tail[8:9]

            def down(s, run):
                outb[s] = run.astype(BF16)
                return gain(s) * run + inbox[s, 0:64, :].astype(F32)

            lax.fori_loop(0, NSEQ, down, jnp.zeros((64, 128), F32))

            def up(k, run):
                s = NSEQ - 1 - k
                outb[s] = jnp.where(lane < STATE, outb[s].astype(F32), run).astype(BF16)
                return gain(s) * run + inbox[s, 0:64, :].astype(F32)

            lax.fori_loop(0, NSEQ, up, jnp.zeros((64, 128), F32))

            def send_second(k, carry):
                second(lax.rem(me + k, NSEQ), me).start()
                return carry

            lax.fori_loop(1, NSEQ, send_second, 0)
            landed[me] = outb[me]

        def finish(k, carry):
            peer = lax.rem(me + k, NSEQ)

            @pl.when(peer < NH)
            def _():
                first(peer, me).wait_send()
                second(me, peer).wait_recv()

            return carry

        lax.fori_loop(1, NSEQ, finish, 0)

        @pl.when(me < NH)
        def _():
            def drain(k, carry):
                second(lax.rem(me + k, NSEQ), me).wait_send()
                return carry

            lax.fori_loop(1, NSEQ, drain, 0)

        for e in range(NH):
            st_out[64 * e : 64 * e + 64, :] = landed[e]
        tail_copy.wait_send()
        stay(kvp, kv_out, 0).wait()
        stay(qdp, qd_out, 1).wait()
        for k in range(RING):
            halo_copy(k).wait()
            if k:
                own_copy(k, kvp, kv_out, ks, kr).wait()
                own_copy(k, qdp, qd_out, qs, qr).wait()


def whole_spec(shape):
    return pl.BlockSpec(shape, lambda i: (0,) * len(shape))


def mixer_specs():
    tok = pl.BlockSpec((T, 128), lambda i: (0, i))
    return [
        tok,
        tok,
        tok,
        pl.BlockSpec((4, 128), lambda i: (0, i)),
        whole_spec((T, NH)),
        whole_spec((1, NH)),
        whole_spec((1, NH)),
        whole_spec((8, T)),
        whole_spec((T, 128)),
        whole_spec((T, 128)),
    ]


DMA = pltpu.SemaphoreType.DMA
WIDTH = NH * 64
ANY = pl.BlockSpec(memory_space=pl.ANY)


def front(shared, queries, keys, values, attn_grad):
    chan = pl.BlockSpec((128, T), lambda i: (i, 0))
    piece = jax.ShapeDtypeStruct((RING, 2, HEAD_DIM, T), BF16)
    return pl.pallas_call(
        front_kernel,
        grid=(PAIRS,),
        in_specs=mixer_specs()
        + [whole_spec((T, 4 * HEAD_DIM))] * 4
        + [pl.BlockSpec((16, WIDTH), lambda i: (T // 16 - 1, 0))],
        out_specs=[chan, chan, whole_spec((WIDTH, 128)), whole_spec((16, WIDTH)), ANY, ANY, ANY],
        out_shape=[
            jax.ShapeDtypeStruct((WIDTH, T), F32),
            jax.ShapeDtypeStruct((WIDTH, T), F32),
            jax.ShapeDtypeStruct((WIDTH, 128), BF16),
            jax.ShapeDtypeStruct((16, WIDTH), BF16),
            piece,
            piece,
            piece,
        ],
        scratch_shapes=[
            VM((5, 32, T), F32),
            VM((T, T), F32),
            VM((T, 128), F32),
            VM((3, T, 128), F32),
            VM((8 + T, 128), F32),
            VM((T, STATE), BF16),
            VM((T, STATE), BF16),
            VM((RING, 2, HEAD_DIM, T), BF16),
            VM((RING, 2, HEAD_DIM, T), BF16),
            VM((4 * HEAD_DIM, T), BF16),
            VM((16, WIDTH), BF16),
            VM((NH, 80, 128), BF16),
            VM((NSEQ, 80, 128), BF16),
            VM((NSEQ, 64, 128), BF16),
            VM((NH, 64, 128), BF16),
            DMA((RING,)), DMA((RING,)), DMA((RING,)), DMA((RING,)), DMA((RING,)), DMA((RING,)),
            DMA, DMA, DMA((2,)), DMA((NSEQ,)), DMA((NSEQ,)), DMA((NSEQ,)), DMA((NSEQ,)),
        ],
        compiler_params=pltpu.CompilerParams(collective_id=1, has_side_effects=True),
        name="front",
        cost_estimate=pl.CostEstimate(
            flops=600000000, bytes_accessed=12000000, transcendentals=1000000
        ),
    )(*shared, queries, keys, values, attn_grad, shared[0])


def rear_kernel(
    conv_ref, gate_ref, mix_ref, w_ref, raw_ref, bias_ref, rate_ref, docc_ref, bin_ref, cout_ref,
    act_ref, g_ref, st_ref, skip_ref, tail_ref, own_ref, back_ref,
    dconv_out, dgate_out, step_out, dw_out, sc_out, gin_out, gout_out, gq_out, gk_out, gv_out,
    rows, tri, scr, mk, xs, bg, cg, bias_m, pair_t, dpair, dcum, ddir, dskp, dbt, dct, qs,
    last, spill, spin, red, inbox, tot, coef_ref, cin, own_in, back_in, fscr,
    bs, br, os, orr, s1, r1, s2, r2, s3, r3, s4, r4,
):
    pair = pl.program_id(0)
    me = lax.axis_index("seq")
    hd = lax.axis_index("head")
    x_me = lax.rem(me, RING)
    base = me - x_me
    bwd = lax.rem(base + NSEQ - RING, NSEQ)

    def back_copy(k):
        return seq_copy(
            back_ref.at[k], back_in.at[k], bs.at[k], br.at[k], bwd + lax.rem(x_me + k, RING)
        )

    def own_copy(k):
        return seq_copy(
            own_ref.at[k], own_in.at[k], os.at[k], orr.at[k], base + lax.rem(x_me + k, RING)
        )

    @pl.when(pair == 0)
    def _():
        barrier = pltpu.get_barrier_semaphore()
        greet_seq(barrier, me)
        for k in range(1, 4):
            pl.semaphore_signal(
                barrier, inc=1, device_id={"head": lax.rem(hd + k, 4)}, device_id_type=MESH
            )
        pl.semaphore_wait(barrier, NSEQ + 2)
        for k in range(RING):
            back_copy(k).start()
            if k:
                own_copy(k).start()
        pltpu.make_async_copy(own_ref.at[0], own_in.at[0], os.at[0]).start()
        red[...] = jnp.zeros_like(red)
        mixer_setup(raw_ref, bias_ref, rate_ref, docc_ref, rows, tri, scr, mk)
        group = lax.axis_index("head") // 2
        bf = group_cols(bin_ref, group)
        cf = group_cols(cout_ref, group)
        bg[...] = bf.astype(BF16)
        cg[...] = cf.astype(BF16)
        pair_t[...] = dot(bf, cf, 1, 1, HI)
        doc = docc_ref[0:1, :]
        dcol = col_of(doc, 128)
        dcol = jnp.concatenate([dcol, dcol], axis=1)
        ok = (tri[...] > 0.5) & (dcol == doc)
        bias_m[...] = jnp.where(ok, 0.0, NEG)
        dpair[...] = jnp.zeros_like(dpair)
        dbt[...] = jnp.zeros_like(dbt)
        dct[...] = jnp.zeros_like(dct)
        dcum[...] = jnp.zeros_like(dcum)
        ddir[...] = jnp.zeros_like(ddir)
        dskp[...] = jnp.zeros_like(dskp)
        qs[...] = jnp.zeros_like(qs)

    act_t = act_ref[...]
    g_t = g_ref[...]
    step_p = pair_rows(rows, 0, pair)
    eg_p = pair_rows(rows, 3, pair)
    te_p = pair_rows(rows, 4, pair)
    s_t = act_t * step_p
    s_b = s_t.astype(BF16)
    g_b = g_t.astype(BF16)
    state = st_ref[...]
    start = state[:, 0:STATE]
    end = state[:, STATE:]
    car = dot(start, cg[...], 1, 1) * eg_p
    dste = dot(end, bg[...], 1, 1) * te_p
    dct[...] += dot(start, (g_t * eg_p).astype(BF16), 0, 0)
    dbt[...] += dot(end, (s_t * te_p).astype(BF16), 0, 0)
    se = start.astype(F32) * end.astype(F32)
    lane = lax.broadcasted_iota(jnp.int32, (1, T), 1)
    ys, dss = [], []
    for a in range(2):
        lo = 64 * a
        h = 2 * pair + a
        cum = rows[2, pl.ds(h, 1), :]
        cc = col_of(cum, 128)
        cc = jnp.concatenate([cc, cc], axis=1)
        w = jnp.exp(jnp.minimum(cum - cc, 0.0) + bias_m[...])
        m = pair_t[...] * w
        mb = m.astype(BF16)
        sh = s_b[lo : lo + 64]
        gh = g_b[lo : lo + 64]
        y = dot(sh, mb, 1, 0)
        dsi = dot(gh, mb, 1, 1)
        dm = dot(sh, gh, 0, 0)
        dpair[...] += dm * w
        z = dm * m
        zr = jnp.sum(jnp.transpose(z[:, 0:128] + z[:, 128:]), axis=0, keepdims=True)
        carh = car[lo : lo + 64]
        dsth = dste[lo : lo + 64]
        gt = g_t[lo : lo + 64]
        st = s_t[lo : lo + 64]
        at = act_t[lo : lo + 64]
        v = jnp.sum(st * dsth, axis=0, keepdims=True)
        d = jnp.sum(z, axis=0, keepdims=True) - zr + jnp.sum(gt * carh, axis=0, keepdims=True) - v
        thr = rows[3, pl.ds(h, 1), :][:, T - 1 : T]
        extra = jnp.sum(v, axis=1, keepdims=True) + thr * jnp.sum(
            jnp.sum(se[lo : lo + 64], axis=0, keepdims=True), axis=1, keepdims=True
        )
        dcum[pl.ds(h, 1), :] = d + jnp.where(lane == T - 1, extra, 0.0)
        ds = dsi + dsth
        ddir[pl.ds(h, 1), :] = jnp.sum(ds * at, axis=0, keepdims=True)
        dskp[pl.ds(h, 1), :] = jnp.sum(gt * at, axis=0, keepdims=True)
        skip = skip_ref[h]
        ys.append(y + carh + skip * at)
        dss.append(ds * step_p[lo : lo + 64] + skip * gt)
    y = jnp.transpose(jnp.concatenate(ys, axis=0))
    dact = jnp.transpose(jnp.concatenate(dss, axis=0))
    gate = gate_ref[...].astype(F32)
    sg = sigmoid(gate)
    dgate_out[...] = (
        mix_ref[...].astype(F32) * y * (sg * (1.0 + gate * (1.0 - sg)))
    ).astype(BF16)
    x = conv_ref[...].astype(F32)
    pre = conv_forward(x, tail_rows(tail_ref, pair), w_ref, mk, xs)
    sp = sigmoid(pre)
    dpre = dact * (sp * (1.0 + pre * (1.0 - sp)))
    dx = None
    for k in range(4):
        q = dpre if k == 0 else dpre * mk[k - 1]
        red[pair, k : k + 1, :] = jnp.sum(q * xs[8 - k : 8 - k + T, :], axis=0, keepdims=True)
        qs[8 : 8 + T, :] = q
        term = w_ref[k : k + 1, :] * qs[k : k + 8 + T, :]
        dx = term if dx is None else dx + term
    lanes = pl.ds(pl.multiple_of(pair * 128, 128), 128)
    spill[:, lanes] = dx[0:8]
    dconv_out[:, lanes] = dx[8:].astype(BF16)
    last[:, lanes] = dx[T - 8 :]

    @pl.when(pair == PAIRS - 1)
    def _():
        dld = dot(dcum[...], tri[...], 1, 1, HI)
        zero = jnp.zeros((96, T), F32)
        to_tok = lambda v: jnp.transpose(jnp.concatenate([v, zero], axis=0))[:, 0:NH]
        dld_t = to_tok(dld)
        dir_t = to_tok(ddir[...])
        rate = jnp.exp(rate_ref[...])
        v = raw_ref[...] + bias_ref[...]
        step = jnp.log(1.0 + jnp.exp(v))
        gs = (dir_t - dld_t * rate) * sigmoid(v)
        step_out[...] = gs
        red[PAIRS, 0:1, 0:NH] = jnp.sum(gs, axis=0, keepdims=True)
        red[PAIRS, 1:2, 0:NH] = -rate * jnp.sum(dld_t * step, axis=0, keepdims=True)
        red[PAIRS, 2:3, 0:NH] = jnp.sum(to_tok(dskp[...]), axis=0, keepdims=True)
        dp = dpair[...].astype(BF16)
        coef_ref[0:STATE] = (dbt[...] + dot(jnp.transpose(cg[...].astype(F32)).astype(BF16), dp, 1, 1)).astype(BF16)
        coef_ref[STATE:] = (dct[...] + dot(jnp.transpose(bg[...].astype(F32)).astype(BF16), dp, 1, 0)).astype(BF16)

        def coef(k, frm):
            return pltpu.make_async_remote_copy(
                src_ref=coef_ref,
                dst_ref=cin.at[frm],
                send_sem=s3.at[k],
                recv_sem=r3.at[frm],
                device_id={"head": lax.rem(hd + k, 4)},
                device_id_type=MESH,
            )

        spill_copy = seq_copy(spill, spin, s4, r4, lax.rem(me + NSEQ - 1, NSEQ))

        def first(block, frm):
            return seq_copy(red.at[block], inbox.at[frm], s1.at[block], r1.at[frm], 2 * block)

        def second(peer, block):
            return seq_copy(tot.at[block], tot.at[block], s2.at[peer], r2.at[block], peer)

        def send_first(b, carry):
            @pl.when(2 * b != me)
            def _():
                first(b, me).start()

            return carry

        lax.fori_loop(0, BLOCKS, send_first, 0)
        for k in range(1, 4):
            coef(k, hd).start()
        spill_copy.start()
        mine = me // 2
        owner = (me == 2 * mine) & (mine < BLOCKS)

        @pl.when(owner)
        def _():
            inbox[me] = red[mine]

            def wait_first(k, carry):
                first(mine, lax.rem(me + k, NSEQ)).wait_recv()
                return carry

            lax.fori_loop(1, NSEQ, wait_first, 0)
            tot[mine] = jnp.sum(inbox[...], axis=0)

            def send_second(k, carry):
                second(lax.rem(me + k, NSEQ), mine).start()
                return carry

            lax.fori_loop(1, NSEQ, send_second, 0)

        for k in range(1, 4):
            coef(k, lax.rem(hd + k, 4)).wait_recv()
        cin[hd] = coef_ref[...]
        g0 = jnp.transpose(cin[0].astype(F32) + cin[1].astype(F32))
        g1 = jnp.transpose(cin[2].astype(F32) + cin[3].astype(F32))
        gin_out[...] = jnp.concatenate([g0[:, 0:STATE], g1[:, 0:STATE]], axis=1)
        gout_out[...] = jnp.concatenate([g0[:, STATE:], g1[:, STATE:]], axis=1)
        spill_copy.wait_recv()
        fixed = jnp.concatenate([last[0:8, :], last[8:16, :] + spin[...]], axis=0)
        dconv_out[T - 16 :, :] = fixed.astype(BF16)
        pltpu.make_async_copy(own_ref.at[0], own_in.at[0], os.at[0]).wait()
        for k in range(RING):
            if k:
                own_copy(k).wait()
            back_copy(k).wait()
        for slot, dest in enumerate((gq_out, gk_out, gv_out)):
            for k in range(RING):
                h = lax.rem(x_me - k + RING, RING)
                part = own_in[k, slot].astype(F32)
                if slot:
                    part = part + back_in[k, slot - 1].astype(F32)
                fscr[pl.ds(pl.multiple_of(h * HEAD_DIM, 32), HEAD_DIM), :] = part
            dest[...] = jnp.transpose(fscr[...]).astype(BF16)

        def wait_second(b, carry):
            @pl.when(2 * b != me)
            def _():
                second(me, b).wait_recv()
                first(b, me).wait_send()

            return carry

        lax.fori_loop(0, BLOCKS, wait_second, 0)
        for p in range(PAIRS):
            dw_out[:, 128 * p : 128 * p + 128] = tot[p, 0:4, :]
        sc_out[...] = tot[PAIRS]

        @pl.when(owner)
        def _():
            def drain(k, carry):
                second(lax.rem(me + k, NSEQ), mine).wait_send()
                return carry

            lax.fori_loop(1, NSEQ, drain, 0)

        for k in range(1, 4):
            coef(k, hd).wait_send()
        spill_copy.wait_send()


BLOCKS = PAIRS + 1


def rear(shared, act_t, g_t, states, skip, tail, own, back):
    tok = pl.BlockSpec((T, 128), lambda i: (0, i))
    chan = pl.BlockSpec((128, T), lambda i: (i, 0))
    piece = jax.ShapeDtypeStruct((T, 4 * HEAD_DIM), BF16)
    outs = [
        jax.ShapeDtypeStruct((T, WIDTH), BF16),
        jax.ShapeDtypeStruct((T, WIDTH), BF16),
        jax.ShapeDtypeStruct((T, NH), F32),
        jax.ShapeDtypeStruct((4, WIDTH), F32),
        jax.ShapeDtypeStruct((8, 128), F32),
        jax.ShapeDtypeStruct((T, 128), F32),
        jax.ShapeDtypeStruct((T, 128), F32),
        piece,
        piece,
        piece,
    ]
    specs = [whole_spec(o.shape) for o in outs]
    specs[1] = tok
    return pl.pallas_call(
        rear_kernel,
        grid=(PAIRS,),
        in_specs=mixer_specs()
        + [
            chan,
            chan,
            pl.BlockSpec((128, 128), lambda i: (i, 0)),
            pl.BlockSpec(memory_space=pltpu.SMEM),
            whole_spec((16, WIDTH)),
            ANY,
            ANY,
        ],
        out_specs=specs,
        out_shape=outs,
        scratch_shapes=[
            VM((5, 32, T), F32),
            VM((T, T), F32),
            VM((T, 128), F32),
            VM((3, T, 128), F32),
            VM((8 + T, 128), F32),
            VM((T, STATE), BF16),
            VM((T, STATE), BF16),
            VM((T, T), F32),
            VM((T, T), F32),
            VM((T, T), F32),
            VM((32, T), F32),
            VM((32, T), F32),
            VM((32, T), F32),
            VM((STATE, T), F32),
            VM((STATE, T), F32),
            VM((16 + T, 128), F32),
            VM((16, WIDTH), F32),
            VM((8, WIDTH), F32),
            VM((8, WIDTH), F32),
            VM((BLOCKS, 8, 128), F32),
            VM((NSEQ, 8, 128), F32),
            VM((BLOCKS, 8, 128), F32),
            VM((128, T), BF16),
            VM((4, 128, T), BF16),
            VM((RING, 3, HEAD_DIM, T), BF16),
            VM((RING, 2, HEAD_DIM, T), BF16),
            VM((4 * HEAD_DIM, T), F32),
            DMA((RING,)), DMA((RING,)), DMA((RING,)), DMA((RING,)),
            DMA((BLOCKS,)), DMA((NSEQ,)), DMA((NSEQ,)), DMA((BLOCKS,)),
            DMA((4,)), DMA((4,)), DMA, DMA,
        ],
        compiler_params=pltpu.CompilerParams(collective_id=2, has_side_effects=True),
        name="rear",
        cost_estimate=pl.CostEstimate(
            flops=3000000000, bytes_accessed=10000000, transcendentals=3000000
        ),
    )(*shared, act_t, g_t, states, skip, tail, own, back)


def local(
    queries, keys, values, attn_grad, doc_ids, conv_input, conv_weight, step_raw, step_bias,
    rate_log, skip_gain, input_coeff, output_coeff, gate_input, mix_grad,
):
    me = lax.axis_index("seq")
    doc_pad = jnp.concatenate([jnp.full((WINDOW,), -1, jnp.int32), doc_ids])
    doc_rows = lax.dynamic_slice_in_dim(doc_pad, me // RING * WINDOW, 2 * WINDOW)
    doc_rows = doc_rows.reshape(8, T).astype(F32)
    ext = lax.dynamic_slice_in_dim(doc_pad, me * T + WINDOW - 3, T + 3)
    doc = ext[3:]
    docc = jnp.stack(
        [doc, doc == ext[2], doc == doc[T - 1]]
        + [doc == ext[3 - k : 3 - k + T] for k in range(1, 4)]
        + [doc, doc]
    ).astype(F32)
    shared = (
        conv_input, gate_input, mix_grad, conv_weight, step_raw, step_bias[None], rate_log[None],
        docc, input_coeff, output_coeff,
    )
    act_t, g_t, states, tail, kv, qd, halo = front(shared, queries, keys, values, attn_grad)
    own, back = attn_core(kv, qd, halo, doc_rows)
    dconv, dgate, gstep, dw, sc, gin, gout, gq, gk, gv = rear(
        shared, act_t, g_t, states, skip_gain, tail, own, back
    )
    return (
        gq, gk, gv, dconv, dgate, gstep, gin, gout, dw, sc[0, :NH], sc[1, :NH], sc[2, :NH]
    )


def solution(mesh):
    both = P("seq", "head")
    return jax.shard_map(
        local,
        mesh=mesh,
        in_specs=(
            both, both, both, both, P(), both, P(None, "head"), both, P("head"), P("head"),
            P("head"), P("seq", None), P("seq", None), both, both,
        ),
        out_specs=(
            both, both, both, both, both, both, P("seq", None), P("seq", None),
            P(None, "head"), P("head"), P("head"), P("head"),
        ),
        check_vma=False,
    )
```

time: 177 us -> 147 us (0.83)
  starting transfers between devices: 43.3 us -> 0 us
  Pallas kernels: 101 us -> 127 us
  waiting for transfers between devices: 15.5 us -> 0 us
  local copies, waits for them, and re-layouts: 9.76 us -> 14.8 us
    ppermute x18 -> x0, starting transfers between devices: 43.3 us -> none  [the longest x8 25 us: group_shift(): return lax.ppermute(value, 'seq', pairs)]
    pallas_call x7 -> x3, Pallas kernels: 101 us -> 127 us  [the longest x1 62.9 us: front(): pl.pallas_call(front_kernel, grid=(PAIRS,), in_specs=mixer_specs() + [who...]
    ppermute x18 -> x0, waiting for transfers between devices: 15.5 us -> none  [the longest x8 15.5 us: group_shift(): return lax.ppermute(value, 'seq', pairs)]
    unnamed x57 -> x22, local copies, waits for them, and re-layouts: 6.32 us -> 11.4 us
  transfers between devices with their start and end apart: 18 -> 0, of which waited for: 2 -> 0; matrix products, arithmetic and copies ran while one was open for 5% -> 0% of each run, Pallas kernels for 50% -> 0%
where the time goes in v1:
time: 147 us; the launch traced here: 146 us
  Pallas kernels  127 us (86%)
  local copies, waits for them, and re-layouts  14.8 us (10%)
  other arithmetic  2.66 us (2%)
    pallas_call x1, Pallas kernels, front(): pl.pallas_call(front_kernel, grid=(PAIRS,), in_specs=mixer_specs() + [who...  62.9 us
    pallas_call x1, Pallas kernels, rear(): pl.pallas_call(rear_kernel, grid=(PAIRS,), in_specs=mixer_specs() + [chan...  54.2 us
    unnamed x22, local copies, waits for them, and re-layouts  11.4 us
    pallas_call x1, Pallas kernels, attn_core(): pl.pallas_call(attn_kernel, out_shape=[jax.ShapeDtypeStruct((RING, 3, HEA...  10.3 us

profile of v1, /device:TPU:0, one launch (start us, length us, event | category | flops | bytes accessed | tf_op | source)
XLA Modules:
  0.0 145.5 jit_solution(1715409222439919416)
XLA Ops:
  0.7 0.8 pad_dynamic-slice_fusion.1
  1.4 0.1 slice.28
  1.5 0.6 fusion.1
  2.1 1.4 compare_convert_fusion
  3.5 0.6 convert_element_type.6.docc_ref
  4.1 0.7 fusion
  4.8 0.6 convert_element_type.15.refs_3_
  5.4 1.5 %copy.28.raw_ref = f32[256,28]{1,0:T(8,128)} copy(f32[256,28]{0,1:T(8,128)} %param.22) | data formatting | bytes 57344 | tf_op args[7]
  6.9 62.9 %front.1 = (f32[1792,256]{1,0:T(8,128)}, f32[1792,256]{1,0:T(8,128)}, bf16[1792,128]{1,0:T(8,128)(2,1)}, bf16[16,1792]{1,0:T(8,128)(2,1)}, bf16[4,2,224,256]{3,2...) custom-call(bf16[256,1792]{1,0:T(8,128)(2,1)} %conv_ref.3, ...), custom_call_target="tpu_custom_call" | custom-call | flops 600000000 | bytes 12000000 | tf_op jit(solution)/shard_map/front/pallas_call | solution.py:391
  69.8 10.3 %attn_core.1 = (bf16[4,3,224,256]{3,2,1,0:T(8,128)(2,1)}, bf16[4,2,224,256]{3,2,1,0:T(8,128)(2,1)}) custom-call(bf16[4,2,224,256]{3,2,1,0:T(8,128)(2,1)} %get-tuple-element.35.refs_0_, bf16[4,2,224,256]{3,2,1,0:T(8,128)(2,1)} %get-tuple-element.36.refs_1_, bf16[4,2,224,256]{3,2,1,0:T(8,128)(2,1)} %get-tuple-element.37.refs_2_, ...), custom_call_target="tpu_custom_call" | custom-call | flops 3000000000 | bytes 8000000 | tf_op jit(solution)/shard_map/attn_core/pallas_call | solution.py:113
  80.1 54.2 %rear.1 = (bf16[256,1792]{1,0:T(8,128)(2,1)}, bf16[256,1792]{1,0:T(8,128)(2,1)}, f32[256,28]{1,0:T(8,128)}, f32[4,1792]{1,0:T(4,128)}, f32[8,128]{1,0:T(8,128)},...) custom-call(bf16[256,1792]{1,0:T(8,128)(2,1)} %conv_ref.3, ...), custom_call_target="tpu_custom_call" | custom-call | flops 3000000000 | bytes 10000000 | tf_op jit(solution)/shard_map/rear/pallas_call | solution.py:709
  134.3 0.0 copy-start.2
  134.3 0.0 copy-start.1
  134.3 1.3 slice_bitcast_fusion
  135.6 1.6 %copy.29 = f32[256,28]{0,1:T(8,128)} copy(f32[256,28]{1,0:T(8,128)} %get-tuple-element.55) | data formatting | bytes 57344
  137.2 1.8 %copy.38 = bf16[256,896]{1,0:T(8,128)(2,1)} copy(bf16[256,896]{1,0:T(8,128)(2,1)} %get-tuple-element.84) | data formatting | bytes 917504
  139.0 0.0 copy-start
  139.0 1.9 %copy.39 = bf16[256,896]{1,0:T(8,128)(2,1)} copy(bf16[256,896]{1,0:T(8,128)(2,1)} %get-tuple-element.85) | data formatting | bytes 917504
  140.9 0.0 copy-done.2
  140.9 0.8 copy.40
  141.7 0.0 copy-done.1
  141.7 0.0 copy-start.4
  141.7 0.0 copy-start.3
  141.7 0.9 copy.41
  142.7 0.0 copy-done
  142.7 0.9 copy.42
  143.6 0.0 copy-done.4
  143.6 0.7 copy.43
  144.2 0.0 copy-done.3
  144.2 0.7 copy.44
  144.9 0.0 copy-done.5
  144.9 0.6 copy.45
  (2 shorter events, 0.0 us)
Async XLA Ops:
  134.3 6.7 %copy-start.2 = (bf16[256,896]{1,0:T(8,128)(2,1)S(1)}, bf16[256,896]{1,0:T(8,128)(2,1)}, u32[]{:S(2)}) copy-start(bf16[256,896]{1,0:T(8,128)(2,1)} %get-tuple-element.86) | copy-start | bytes 1376260
  134.3 7.4 %copy-start.1 = (bf16[256,1792]{1,0:T(8,128)(2,1)S(1)}, bf16[256,1792]{1,0:T(8,128)(2,1)}, u32[]{:S(2)}) copy-start(bf16[256,1792]{1,0:T(8,128)(2,1)} %get-tuple-element.87) | copy-start | bytes 2752516
  139.0 3.6 %copy-start = (bf16[256,1792]{1,0:T(8,128)(2,1)S(1)}, bf16[256,1792]{1,0:T(8,128)(2,1)}, u32[]{:S(2)}) copy-start(bf16[256,1792]{1,0:T(8,128)(2,1)} %get-tuple-element.88) | copy-start | bytes 2752516
  141.7 1.9 %copy-start.4 = (f32[256,128]{1,0:T(8,128)S(1)}, f32[256,128]{1,0:T(8,128)}, u32[]{:S(2)}) copy-start(f32[256,128]{1,0:T(8,128)} %get-tuple-element.90) | copy-start | bytes 393220
  141.7 2.5 %copy-start.3 = (f32[256,128]{1,0:T(8,128)S(1)}, f32[256,128]{1,0:T(8,128)}, u32[]{:S(2)}) copy-start(f32[256,128]{1,0:T(8,128)} %get-tuple-element.91) | copy-start | bytes 393220
  141.7 3.2 %copy-start.5 = (f32[4,1792]{1,0:T(4,128)S(1)}, f32[4,1792]{1,0:T(4,128)}, u32[]{:S(2)}) copy-start(f32[4,1792]{1,0:T(4,128)} %get-tuple-element.92) | copy-start | bytes 86020

commit v2 on v1

v2 whole, which is shorter than its diff:
```python
import jax
import jax.numpy as jnp
from jax import lax
from jax.experimental import pallas as pl
from jax.experimental.pallas import tpu as pltpu
from jax.sharding import PartitionSpec as P

HEAD_DIM = 224
WINDOW = 1024
SSM_HEADS = 112
STATE = 64
GROUPS = 2
T = 256
NH = 28
PAIRS = 14
NSEQ = 32
RING = 4
NEG = -1e30
F32 = jnp.float32
BF16 = jnp.bfloat16
MESH = pl.DeviceIdType.MESH
VM = pltpu.VMEM
SCALE = HEAD_DIM ** (-0.5)
HI = lax.Precision.HIGHEST


def dot(a, b, ca, cb, precision=None):
    return lax.dot_general(
        a, b, (((ca,), (cb,)), ((), ())), preferred_element_type=F32, precision=precision
    )


def sigmoid(v):
    return 1.0 / (1.0 + jnp.exp(-v))


def col_of(row, rows):
    return jnp.transpose(jnp.broadcast_to(row, (rows, row.shape[1])))


DMA = pltpu.SemaphoreType.DMA
WIDTH = NH * 64
BLOCKS = PAIRS + 1
ANY = pl.BlockSpec(memory_space=pl.ANY)


def doc_row(ref, shard):
    safe = jnp.maximum(shard, 0) * 2
    row = jnp.concatenate([ref[pl.ds(safe, 1), :], ref[pl.ds(safe + 1, 1), :]], axis=1)
    return jnp.where(shard < 0, -1.0, row.astype(F32))


def mixer_setup(me, raw_ref, bias_ref, rate_ref, doc_ref, drows, rows, tri, mk, vcol, small):
    base = me - lax.rem(me, RING)
    for c in range(2 * RING):
        drows[c : c + 1, :] = doc_row(doc_ref, base - RING + c)
    doc = doc_row(doc_ref, me)
    prev = doc_row(doc_ref, me - 1)
    small[...] = jnp.zeros_like(small)
    small[0:1, 0:NH] = bias_ref[...]
    small[1:2, 0:NH] = jnp.exp(rate_ref[...])
    bias = col_of(small[0:1, :], 128)[0:NH]
    rate = col_of(small[1:2, :], 128)[0:NH]
    vcol[...] = jnp.concatenate([rate, rate], axis=1)
    rows[...] = jnp.zeros_like(rows)
    step = jnp.log(1.0 + jnp.exp(raw_ref[...] + jnp.concatenate([bias, bias], axis=1)))
    rows[0, 0:NH, :] = step
    rows[1, 0:NH, :] = -step * vcol[...]
    i = lax.broadcasted_iota(jnp.int32, (T, T), 0)
    j = lax.broadcasted_iota(jnp.int32, (T, T), 1)
    tri[...] = jnp.where(i <= j, 1.0, 0.0)
    cum = dot(rows[1], tri[...], 1, 0, HI)
    rows[2] = cum
    rows[3] = jnp.where(doc == prev[:, T - 1 : T], jnp.exp(cum), 0.0)
    rows[4] = jnp.where(
        doc == doc[:, T - 1 : T], jnp.exp(jnp.minimum(cum[:, T - 1 : T] - cum, 0.0)), 0.0
    )
    lane = lax.broadcasted_iota(jnp.int32, (8, T), 1)
    doc8 = jnp.broadcast_to(doc, (8, T))
    prev8 = jnp.broadcast_to(prev, (8, T))
    for k in range(1, 4):
        lag = jnp.where(lane < k, pltpu.roll(prev8, k, 1), pltpu.roll(doc8, k, 1))
        mk[k - 1] = col_of(jnp.where(lag == doc8, 1.0, 0.0)[0:1, :], 128)


def pair_rows(rows, which, pair):
    a = rows[which, pl.ds(2 * pair, 1), :]
    b = rows[which, pl.ds(2 * pair + 1, 1), :]
    return jnp.concatenate(
        [jnp.broadcast_to(a, (64, T)), jnp.broadcast_to(b, (64, T))], axis=0
    )


def group_cols(ref, group):
    v = ref[...].astype(F32)
    return jnp.where(group == 0, v[:, 0:STATE], v[:, STATE:])


def conv_forward(x, tail, w_ref, mk, xs):
    xs[0:8, :] = tail
    xs[8 : 8 + T, :] = x
    pre = w_ref[0:1, :] * x
    for k in range(1, 4):
        pre = pre + w_ref[k : k + 1, :] * (mk[k - 1] * xs[8 - k : 8 - k + T, :])
    return pre


def tail_rows(ref, pair):
    lanes = pl.ds(pl.multiple_of(pair * 128, 128), 128)
    return ref[:, lanes].astype(F32)[8:16]


def seq_copy(src, dst, send, recv, peer):
    return pltpu.make_async_remote_copy(
        src_ref=src,
        dst_ref=dst,
        send_sem=send,
        recv_sem=recv,
        device_id={"seq": peer},
        device_id_type=MESH,
    )


def greet_seq(barrier, me):
    def greet(k, carry):
        peer = lax.rem(me + k, NSEQ)
        pl.semaphore_signal(barrier, inc=1, device_id={"seq": peer}, device_id_type=MESH)
        return carry

    lax.fori_loop(1, NSEQ, greet, 0)


def attention(x_me, kva, qda, drows, dka, dva, dq_out, send_dq):
    dka[...] = jnp.zeros_like(dka)
    dva[...] = jnp.zeros_like(dva)
    row_i = lax.broadcasted_iota(jnp.int32, (T, T), 0)
    col_j = lax.broadcasted_iota(jnp.int32, (T, T), 1)

    def chunk(c, carry):
        slot = lax.rem(x_me - c + RING, RING)
        qt = qda[slot, 0]
        gt = qda[slot, 1]
        q = jnp.transpose(qt.astype(F32)).astype(BF16)
        g = jnp.transpose(gt.astype(F32)).astype(BF16)
        dq_col = col_of(drows[pl.ds(RING + c, 1), :], 128)
        dq_col = jnp.concatenate([dq_col, dq_col], axis=1)
        scores, masks, slots = [], [], []
        row_max = None
        for b in range(RING + 1):
            kc = c + b
            slots.append(kc // RING * RING + lax.rem(x_me - kc + 2 * RING, RING))
            s = dot(q, kva[slots[b], 0], 1, 0) * SCALE
            ok = dq_col == drows[pl.ds(kc, 1), :]
            if b == 0:
                ok = ok & (col_j > row_i)
            if b == RING:
                ok = ok & (col_j <= row_i)
            s = jnp.where(ok, s, NEG)
            scores.append(s)
            masks.append(ok)
            m = jnp.max(s, axis=1, keepdims=True)
            row_max = m if row_max is None else jnp.maximum(row_max, m)
        row_sum = None
        for b in range(RING + 1):
            e = jnp.where(masks[b], jnp.exp(scores[b] - row_max), 0.0)
            scores[b] = e
            r = jnp.sum(e, axis=1, keepdims=True)
            row_sum = r if row_sum is None else row_sum + r
        inv = 1.0 / jnp.maximum(row_sum, 1.0)
        dprobs = []
        delta = None
        for b in range(RING + 1):
            p = scores[b] * inv
            scores[b] = p
            half = p.astype(BF16)
            dp = dot(g, kva[slots[b], 1], 1, 0)
            dprobs.append(dp)
            r = jnp.sum(half.astype(F32) * dp, axis=1, keepdims=True)
            delta = r if delta is None else delta + r
            dva[c + b] = dva[c + b] + dot(gt, half, 1, 0)
        dqt = None
        for b in range(RING + 1):
            ds = (scores[b] * (dprobs[b] - delta)).astype(BF16)
            r = dot(kva[slots[b], 0], ds, 1, 1)
            dqt = r if dqt is None else dqt + r
            dka[c + b] = dka[c + b] + dot(qt, ds, 1, 0)
        k = lax.rem(c - x_me + RING, RING)
        dq_out[k] = (dqt * SCALE).astype(BF16)
        send_dq(k)
        return carry

    lax.fori_loop(0, RING, chunk, 0)


def layer_kernel(
    conv_ref, gate_ref, mix_ref, w_ref, raw_ref, bias_ref, rate_ref, doc_ref, bin_ref, cout_ref,
    q_ref, k_ref, v_ref, do_ref, edge_ref, skip_ref,
    dconv_out, dgate_out, step_out, dw_out, sc_out, gin_out, gout_out, gq_out, gk_out, gv_out,
    drows, rows, tri, mk, vcol, small, xs, bg, cg, act_s, g_s,
    kvp, qdp, tscr, kva, qda, tail_in, pay, inbox, outb, landed,
    dka, dva, dq_out, own_out, back_out, dq_in, own_in, back_in, fscr,
    bias_m, pair_t, dpair, dcum, ddir, dskp, dbt, dct, qs,
    last, spill, spin, red, rinbox, tot, coef_ref, cin,
    hs, hr, ks, kr, qsm, qr, ts, tr, cs1, cr1, cs2, cr2,
    ds_, dr, osm, orr, bs, br, s1, r1, s2, r2, s3, r3, s4, r4,
):
    step_id = pl.program_id(0)
    pair = lax.rem(step_id, PAIRS)
    me = lax.axis_index("seq")
    hd = lax.axis_index("head")
    x_me = lax.rem(me, RING)
    base = me - x_me
    fwd = lax.rem(base + RING, NSEQ)
    bwd = lax.rem(base + NSEQ - RING, NSEQ)

    def near(k):
        return base + lax.rem(x_me + k, RING)

    def halo_copy(k):
        return seq_copy(kva.at[RING + k], kva.at[k], hs.at[k], hr.at[k], fwd + x_me)

    def kv_copy(k):
        return seq_copy(kvp.at[k], kva.at[RING + k], ks.at[k], kr.at[k], near(k))

    def qd_copy(k):
        return seq_copy(qdp.at[k], qda.at[k], qsm.at[k], qr.at[k], near(k))

    def dq_copy(k):
        return seq_copy(dq_out.at[k], dq_in.at[k], ds_.at[k], dr.at[k], near(k))

    def own_copy(k):
        return seq_copy(own_out.at[k], own_in.at[k], osm.at[k], orr.at[k], near(k))

    def back_copy(k):
        return seq_copy(
            back_out.at[k], back_in.at[k], bs.at[k], br.at[k], bwd + lax.rem(x_me + k, RING)
        )

    def first_copy(peer, frm):
        return seq_copy(pay.at[peer], inbox.at[frm], cs1.at[peer], cr1.at[frm], peer)

    def second_copy(peer, frm):
        return seq_copy(outb.at[peer], landed.at[frm], cs2.at[peer], cr2.at[frm], peer)

    tail_copy = seq_copy(edge_ref, tail_in, ts, tr, lax.rem(me + 1, NSEQ))

    @pl.when(step_id == 0)
    def _():
        barrier = pltpu.get_barrier_semaphore()
        greet_seq(barrier, me)
        for k in range(1, 4):
            pl.semaphore_signal(
                barrier, inc=1, device_id={"head": lax.rem(hd + k, 4)}, device_id_type=MESH
            )

        def prepare(src, dest, landing, slot):
            tscr[...] = jnp.transpose(src[...].astype(F32)).astype(BF16)
            for k in range(RING):
                h = lax.rem(x_me + k, RING)
                part = tscr[pl.ds(pl.multiple_of(h * HEAD_DIM, 32), HEAD_DIM), :]
                if k:
                    dest[k, slot] = part
                else:
                    landing[slot] = part

        prepare(k_ref, kvp, kva.at[RING], 0)
        prepare(v_ref, kvp, kva.at[RING], 1)
        pl.semaphore_wait(barrier, NSEQ + 2)
        tail_copy.start()
        halo_copy(0).start()
        for k in (1, 3, 2):
            kv_copy(k).start()
        prepare(q_ref, qdp, qda.at[0], 0)
        prepare(do_ref, qdp, qda.at[0], 1)
        for k in (1, 3, 2):
            qd_copy(k).start()
        red[...] = jnp.zeros_like(red)
        mixer_setup(me, raw_ref, bias_ref, rate_ref, doc_ref, drows, rows, tri, mk, vcol, small)
        group = hd // 2
        bf = group_cols(bin_ref, group)
        cf = group_cols(cout_ref, group)
        bg[...] = bf.astype(BF16)
        cg[...] = cf.astype(BF16)
        thr = rows[3][:, T - 1 : T]
        for e in range(NH):
            t = jnp.broadcast_to(thr[e : e + 1, :], (8, 128))
            hi = t.astype(BF16).astype(F32)
            pay[e, 64:80, :] = jnp.concatenate([hi, t - hi], axis=0).astype(BF16)
        pair_t[...] = dot(bf, cf, 1, 1, HI)
        doc = drows[pl.ds(RING + x_me, 1), :]
        dcol = col_of(doc, 128)
        dcol = jnp.concatenate([dcol, dcol], axis=1)
        bias_m[...] = jnp.where((tri[...] > 0.5) & (dcol == doc), 0.0, NEG)
        for ref in (dpair, dbt, dct, dcum, ddir, dskp, qs):
            ref[...] = jnp.zeros_like(ref)
        tail_copy.wait_recv()

    rows128 = pl.ds(pl.multiple_of(pair * 128, 128), 128)

    @pl.when(step_id < PAIRS)
    def _():
        x = conv_ref[...].astype(F32)
        pre = conv_forward(x, tail_rows(tail_in, pair), w_ref, mk, xs)
        act = pre * sigmoid(pre)
        gate = gate_ref[...].astype(F32)
        g = mix_ref[...].astype(F32) * (gate * sigmoid(gate))
        act_t = jnp.transpose(act)
        g_t = jnp.transpose(g)
        act_s[rows128, :] = act_t
        g_s[rows128, :] = g_t
        st = act_t * (pair_rows(rows, 0, pair) * pair_rows(rows, 4, pair))
        ge = g_t * pair_rows(rows, 3, pair)
        both = jnp.concatenate(
            [dot(st.astype(BF16), bg[...], 1, 0), dot(ge.astype(BF16), cg[...], 1, 0)], axis=1
        ).astype(BF16)
        pay[2 * pair, 0:64, :] = both[0:64]
        pay[2 * pair + 1, 0:64, :] = both[64:128]

    @pl.when(step_id == 7)
    def _():
        for k in (1, 3):
            kv_copy(k).wait_recv()
            halo_copy(k).start()

    @pl.when(step_id == PAIRS - 1)
    def _():
        kv_copy(2).wait_recv()
        halo_copy(2).start()

        def send_first(k, carry):
            peer = lax.rem(me + k, NSEQ)

            @pl.when(peer < NH)
            def _():
                first_copy(peer, me).start()

            return carry

        lax.fori_loop(1, NSEQ, send_first, 0)
        for k in range(1, RING):
            qd_copy(k).wait_recv()
        for k in range(RING):
            halo_copy(k).wait_recv()

        def send_dq(k):
            @pl.when(k > 0)
            def _():
                dq_copy(k).start()

        attention(x_me, kva, qda, drows, dka, dva, dq_out, send_dq)

        @pl.when(me < NH)
        def _():
            inbox[me] = pay[me]

            def wait_first(k, carry):
                first_copy(me, lax.rem(me + k, NSEQ)).wait_recv()
                return carry

            lax.fori_loop(1, NSEQ, wait_first, 0)
            lane = lax.broadcasted_iota(jnp.int32, (64, 128), 1)

            def gain(s):
                tail = inbox[s, 64:80, :].astype(F32)
                return tail[0:1] + tail[8:9]

            def down(s, run):
                outb[s] = run.astype(BF16)
                return gain(s) * run + inbox[s, 0:64, :].astype(F32)

            lax.fori_loop(0, NSEQ, down, jnp.zeros((64, 128), F32))

            def up(k, run):
                s = NSEQ - 1 - k
                outb[s] = jnp.where(lane < STATE, outb[s].astype(F32), run).astype(BF16)
                return gain(s) * run + inbox[s, 0:64, :].astype(F32)

            lax.fori_loop(0, NSEQ, up, jnp.zeros((64, 128), F32))

            def send_second(k, carry):
                second_copy(lax.rem(me + k, NSEQ), me).start()
                return carry

            lax.fori_loop(1, NSEQ, send_second, 0)
            landed[me] = outb[me]

        for k in range(RING):
            c = lax.rem(x_me + k, RING)
            back_out[k, 0] = (dka[c] * SCALE).astype(BF16)
            back_out[k, 1] = dva[c].astype(BF16)
            back_copy(k).start()
            own_out[k, 0] = (dka[RING + c] * SCALE).astype(BF16)
            own_out[k, 1] = dva[RING + c].astype(BF16)
            if k:
                own_copy(k).start()

    @pl.when(step_id == PAIRS)
    def _():
        def arrive(k, carry):
            peer = lax.rem(me + k, NSEQ)

            @pl.when(peer < NH)
            def _():
                second_copy(me, peer).wait_recv()

            return carry

        lax.fori_loop(1, NSEQ, arrive, 0)

    @pl.when(step_id >= PAIRS)
    def _():
        act_t = act_s[rows128, :]
        g_t = g_s[rows128, :]
        step_p = pair_rows(rows, 0, pair)
        eg_p = pair_rows(rows, 3, pair)
        te_p = pair_rows(rows, 4, pair)
        s_t = act_t * step_p
        s_b = s_t.astype(BF16)
        g_b = g_t.astype(BF16)
        state = jnp.concatenate([landed[2 * pair], landed[2 * pair + 1]], axis=0)
        start = state[:, 0:STATE]
        end = state[:, STATE:]
        car = dot(start, cg[...], 1, 1) * eg_p
        dste = dot(end, bg[...], 1, 1) * te_p
        dct[...] += dot(start, (g_t * eg_p).astype(BF16), 0, 0)
        dbt[...] += dot(end, (s_t * te_p).astype(BF16), 0, 0)
        se = start.astype(F32) * end.astype(F32)
        lane = lax.broadcasted_iota(jnp.int32, (1, T), 1)
        ys, dss = [], []
        for a in range(2):
            lo = 64 * a
            h = 2 * pair + a
            cum = rows[2, pl.ds(h, 1), :]
            cc = col_of(cum, 128)
            cc = jnp.concatenate([cc, cc], axis=1)
            w = jnp.exp(jnp.minimum(cum - cc, 0.0) + bias_m[...])
            m = pair_t[...] * w
            mb = m.astype(BF16)
            sh = s_b[lo : lo + 64]
            gh = g_b[lo : lo + 64]
            y = dot(sh, mb, 1, 0)
            dsi = dot(gh, mb, 1, 1)
            dm = dot(sh, gh, 0, 0)
            dpair[...] += dm * w
            z = dm * m
            zr = jnp.sum(jnp.transpose(z[:, 0:128] + z[:, 128:]), axis=0, keepdims=True)
            carh = car[lo : lo + 64]
            dsth = dste[lo : lo + 64]
            gt = g_t[lo : lo + 64]
            st = s_t[lo : lo + 64]
            at = act_t[lo : lo + 64]
            v = jnp.sum(st * dsth, axis=0, keepdims=True)
            d = jnp.sum(z, axis=0, keepdims=True) - zr + jnp.sum(gt * carh, axis=0, keepdims=True) - v
            thr = rows[3, pl.ds(h, 1), :][:, T - 1 : T]
            extra = jnp.sum(v, axis=1, keepdims=True) + thr * jnp.sum(
                jnp.sum(se[lo : lo + 64], axis=0, keepdims=True), axis=1, keepdims=True
            )
            dcum[pl.ds(h, 1), :] = d + jnp.where(lane == T - 1, extra, 0.0)
            ds = dsi + dsth
            ddir[pl.ds(h, 1), :] = jnp.sum(ds * at, axis=0, keepdims=True)
            dskp[pl.ds(h, 1), :] = jnp.sum(gt * at, axis=0, keepdims=True)
            skip = skip_ref[h]
            ys.append(y + carh + skip * at)
            dss.append(ds * step_p[lo : lo + 64] + skip * gt)
        y = jnp.transpose(jnp.concatenate(ys, axis=0))
        dact = jnp.transpose(jnp.concatenate(dss, axis=0))
        gate = gate_ref[...].astype(F32)
        sg = sigmoid(gate)
        dgate_out[...] = (
            mix_ref[...].astype(F32) * y * (sg * (1.0 + gate * (1.0 - sg)))
        ).astype(BF16)
        x = conv_ref[...].astype(F32)
        pre = conv_forward(x, tail_rows(tail_in, pair), w_ref, mk, xs)
        sp = sigmoid(pre)
        dpre = dact * (sp * (1.0 + pre * (1.0 - sp)))
        dx = None
        for k in range(4):
            q = dpre if k == 0 else dpre * mk[k - 1]
            red[pair, k : k + 1, :] = jnp.sum(q * xs[8 - k : 8 - k + T, :], axis=0, keepdims=True)
            qs[8 : 8 + T, :] = q
            term = w_ref[k : k + 1, :] * qs[k : k + 8 + T, :]
            dx = term if dx is None else dx + term
        spill[:, rows128] = dx[0:8]
        dconv_out[:, rows128] = dx[8:].astype(BF16)
        last[:, rows128] = dx[T - 8 :]

    @pl.when(step_id == 2 * PAIRS - 1)
    def _():
        dld = dot(dcum[...], tri[...], 1, 1, HI)
        rate = vcol[...]
        small[0:1, 0:NH] = bias_ref[...]
        bias = col_of(small[0:1, :], 128)[0:NH]
        v = raw_ref[...] + jnp.concatenate([bias, bias], axis=1)
        dldn = dld[0:NH]
        gs = (ddir[0:NH, :] - dldn * rate) * sigmoid(v)
        step_out[...] = gs
        pick = lax.broadcasted_iota(jnp.int32, (32, 128), 1)
        total = lambda z: jnp.sum(z, axis=1, keepdims=True)
        fscr[...] = jnp.zeros_like(fscr)
        fscr[0:NH, 0:128] = jnp.where(
            pick[0:NH] == 0,
            total(gs),
            jnp.where(pick[0:NH] == 1, total(dldn * rows[1, 0:NH, :]), total(dskp[0:NH, :])),
        )
        red[PAIRS] = jnp.transpose(fscr[0:128, 0:128])[0:8]
        dp = dpair[...].astype(BF16)
        coef_ref[0:STATE] = (dbt[...] + dot(jnp.transpose(cg[...].astype(F32)).astype(BF16), dp, 1, 1)).astype(BF16)
        coef_ref[STATE:] = (dct[...] + dot(jnp.transpose(bg[...].astype(F32)).astype(BF16), dp, 1, 0)).astype(BF16)

        def coef(k, frm):
            return pltpu.make_async_remote_copy(
                src_ref=coef_ref,
                dst_ref=cin.at[frm],
                send_sem=s3.at[k],
                recv_sem=r3.at[frm],
                device_id={"head": lax.rem(hd + k, 4)},
                device_id_type=MESH,
            )

        spill_copy = seq_copy(spill, spin, s4, r4, lax.rem(me + NSEQ - 1, NSEQ))

        def first(block, frm):
            return seq_copy(red.at[block], rinbox.at[frm], s1.at[block], r1.at[frm], 2 * block)

        def second(peer, block):
            return seq_copy(tot.at[block], tot.at[block], s2.at[peer], r2.at[block], peer)

        def send_first(b, carry):
            @pl.when(2 * b != me)
            def _():
                first(b, me).start()

            return carry

        lax.fori_loop(0, BLOCKS, send_first, 0)
        for k in range(1, 4):
            coef(k, hd).start()
        spill_copy.start()
        for k in range(RING):
            if k:
                dq_copy(k).wait_recv()
            h = lax.rem(x_me - k + RING, RING)
            source = dq_in if k else dq_out
            fscr[pl.ds(pl.multiple_of(h * HEAD_DIM, 32), HEAD_DIM), :] = source[k].astype(F32)
        gq_out[...] = jnp.transpose(fscr[...]).astype(BF16)
        mine = me // 2
        owner = (me == 2 * mine) & (mine < BLOCKS)

        @pl.when(owner)
        def _():
            rinbox[me] = red[mine]

            def wait_first(k, carry):
                first(mine, lax.rem(me + k, NSEQ)).wait_recv()
                return carry

            lax.fori_loop(1, NSEQ, wait_first, 0)
            tot[mine] = jnp.sum(rinbox[...], axis=0)

            def send_second(k, carry):
                second(lax.rem(me + k, NSEQ), mine).start()
                return carry

            lax.fori_loop(1, NSEQ, send_second, 0)

        for k in range(1, 4):
            coef(k, lax.rem(hd + k, 4)).wait_recv()
        cin[hd] = coef_ref[...]
        g0 = jnp.transpose(cin[0].astype(F32) + cin[1].astype(F32))
        g1 = jnp.transpose(cin[2].astype(F32) + cin[3].astype(F32))
        gin_out[...] = jnp.concatenate([g0[:, 0:STATE], g1[:, 0:STATE]], axis=1)
        gout_out[...] = jnp.concatenate([g0[:, STATE:], g1[:, STATE:]], axis=1)
        spill_copy.wait_recv()
        fixed = jnp.concatenate([last[0:8, :], last[8:16, :] + spin[...]], axis=0)
        dconv_out[T - 16 :, :] = fixed.astype(BF16)
        for k in range(RING):
            back_copy(k).wait_recv()
            if k:
                own_copy(k).wait_recv()
        for slot, dest in ((0, gk_out), (1, gv_out)):
            for k in range(RING):
                mine_k = own_in if k else own_out
                h = lax.rem(x_me - k + RING, RING)
                fscr[pl.ds(pl.multiple_of(h * HEAD_DIM, 32), HEAD_DIM), :] = mine_k[
                    k, slot
                ].astype(F32) + back_in[k, slot].astype(F32)
            dest[...] = jnp.transpose(fscr[...]).astype(BF16)

        def wait_second(b, carry):
            @pl.when(2 * b != me)
            def _():
                second(me, b).wait_recv()
                first(b, me).wait_send()

            return carry

        lax.fori_loop(0, BLOCKS, wait_second, 0)
        for p in range(PAIRS):
            dw_out[:, 128 * p : 128 * p + 128] = tot[p, 0:4, :]
        sc_out[...] = tot[PAIRS]

        @pl.when(owner)
        def _():
            def drain(k, carry):
                second(lax.rem(me + k, NSEQ), mine).wait_send()
                return carry

            lax.fori_loop(1, NSEQ, drain, 0)

        for k in range(1, 4):
            coef(k, hd).wait_send()
        spill_copy.wait_send()
        tail_copy.wait_send()
        for k in range(RING):
            halo_copy(k).wait_send()
            back_copy(k).wait_send()
            if k:
                kv_copy(k).wait_send()
                qd_copy(k).wait_send()
                dq_copy(k).wait_send()
                own_copy(k).wait_send()

        def sent_first(k, carry):
            peer = lax.rem(me + k, NSEQ)

            @pl.when(peer < NH)
            def _():
                first_copy(peer, me).wait_send()

            return carry

        lax.fori_loop(1, NSEQ, sent_first, 0)

        @pl.when(me < NH)
        def _():
            def sent_second(k, carry):
                second_copy(lax.rem(me + k, NSEQ), me).wait_send()
                return carry

            lax.fori_loop(1, NSEQ, sent_second, 0)


def whole_spec(shape):
    return pl.BlockSpec(shape, lambda i: (0,) * len(shape))


def layer(
    conv_input, gate_input, mix_grad, conv_weight, raw, bias, rate, docs, bin_, cout,
    queries, keys, values, attn_grad, skip,
):
    tok = pl.BlockSpec((T, 128), lambda i: (0, lax.rem(i, PAIRS)))
    piece = jax.ShapeDtypeStruct((T, 4 * HEAD_DIM), BF16)
    outs = [
        jax.ShapeDtypeStruct((T, WIDTH), BF16),
        jax.ShapeDtypeStruct((T, WIDTH), BF16),
        jax.ShapeDtypeStruct((NH, T), F32),
        jax.ShapeDtypeStruct((4, WIDTH), F32),
        jax.ShapeDtypeStruct((8, 128), F32),
        jax.ShapeDtypeStruct((T, 128), F32),
        jax.ShapeDtypeStruct((T, 128), F32),
        piece,
        piece,
        piece,
    ]
    specs = [whole_spec(o.shape) for o in outs]
    specs[1] = pl.BlockSpec((T, 128), lambda i: (0, jnp.maximum(i - PAIRS, 0)))
    square = VM((T, T), F32)
    heads = VM((32, T), F32)
    return pl.pallas_call(
        layer_kernel,
        grid=(2 * PAIRS,),
        in_specs=[
            tok,
            tok,
            tok,
            pl.BlockSpec((4, 128), lambda i: (0, lax.rem(i, PAIRS))),
            whole_spec((NH, T)),
            whole_spec((1, NH)),
            whole_spec((1, NH)),
            whole_spec((64, 128)),
            whole_spec((T, 128)),
            whole_spec((T, 128)),
        ]
        + [whole_spec((T, 4 * HEAD_DIM))] * 4
        + [
            pl.BlockSpec((16, WIDTH), lambda i: (T // 16 - 1, 0)),
            pl.BlockSpec(memory_space=pltpu.SMEM),
        ],
        out_specs=specs,
        out_shape=outs,
        scratch_shapes=[
            VM((8, T), F32),
            VM((5, 32, T), F32),
            square,
            VM((3, T, 128), F32),
            VM((NH, T), F32),
            VM((8, 128), F32),
            VM((8 + T, 128), F32),
            VM((T, STATE), BF16),
            VM((T, STATE), BF16),
            VM((WIDTH, T), F32),
            VM((WIDTH, T), F32),
            VM((RING, 2, HEAD_DIM, T), BF16),
            VM((RING, 2, HEAD_DIM, T), BF16),
            VM((4 * HEAD_DIM, T), BF16),
            VM((2 * RING, 2, HEAD_DIM, T), BF16),
            VM((RING, 2, HEAD_DIM, T), BF16),
            VM((16, WIDTH), BF16),
            VM((NH, 80, 128), BF16),
            VM((NSEQ, 80, 128), BF16),
            VM((NSEQ, 64, 128), BF16),
            VM((NH, 64, 128), BF16),
            VM((2 * RING, HEAD_DIM, T), F32),
            VM((2 * RING, HEAD_DIM, T), F32),
            VM((RING, HEAD_DIM, T), BF16),
            VM((RING, 2, HEAD_DIM, T), BF16),
            VM((RING, 2, HEAD_DIM, T), BF16),
            VM((RING, HEAD_DIM, T), BF16),
            VM((RING, 2, HEAD_DIM, T), BF16),
            VM((RING, 2, HEAD_DIM, T), BF16),
            VM((4 * HEAD_DIM, T), F32),
            square,
            square,
            square,
            heads,
            heads,
            heads,
            VM((STATE, T), F32),
            VM((STATE, T), F32),
            VM((16 + T, 128), F32),
            VM((16, WIDTH), F32),
            VM((8, WIDTH), F32),
            VM((8, WIDTH), F32),
            VM((BLOCKS, 8, 128), F32),
            VM((NSEQ, 8, 128), F32),
            VM((BLOCKS, 8, 128), F32),
            VM((128, T), BF16),
            VM((4, 128, T), BF16),
            DMA((RING,)), DMA((RING,)), DMA((RING,)), DMA((RING,)), DMA((RING,)), DMA((RING,)),
            DMA, DMA,
            DMA((NSEQ,)), DMA((NSEQ,)), DMA((NSEQ,)), DMA((NSEQ,)),
            DMA((RING,)), DMA((RING,)), DMA((RING,)), DMA((RING,)), DMA((RING,)), DMA((RING,)),
            DMA((BLOCKS,)), DMA((NSEQ,)), DMA((NSEQ,)), DMA((BLOCKS,)),
            DMA((4,)), DMA((4,)), DMA, DMA,
        ],
        compiler_params=pltpu.CompilerParams(
            collective_id=1, has_side_effects=True, vmem_limit_bytes=60 * 1024 * 1024
        ),
        name="layer",
        cost_estimate=pl.CostEstimate(
            flops=6000000000, bytes_accessed=12000000, transcendentals=6000000
        ),
    )(
        conv_input, gate_input, mix_grad, conv_weight, raw, bias, rate, docs, bin_, cout,
        queries, keys, values, attn_grad, conv_input, skip,
    )


def finish_kernel(*refs):
    half = len(refs) // 2
    for src, dest in zip(refs[:half], refs[half:]):
        dest[...] = src[...]


def finish(arrays):
    parts = 7

    def spec(a):
        if a.shape[0] == T and a.shape[1] > 128:
            return pl.BlockSpec((T, a.shape[1] // parts), lambda i: (0, i))
        return whole_spec(a.shape)

    specs = [spec(a) for a in arrays]
    return pl.pallas_call(
        finish_kernel,
        grid=(parts,),
        in_specs=specs,
        out_specs=specs,
        out_shape=[jax.ShapeDtypeStruct(a.shape, a.dtype) for a in arrays],
        compiler_params=pltpu.CompilerParams(vmem_limit_bytes=60 * 1024 * 1024),
        name="finish",
        cost_estimate=pl.CostEstimate(flops=1000000, bytes_accessed=7000000, transcendentals=0),
    )(*arrays)


def local(
    queries, keys, values, attn_grad, doc_ids, conv_input, conv_weight, step_raw, step_bias,
    rate_log, skip_gain, input_coeff, output_coeff, gate_input, mix_grad,
):
    outs = layer(
        conv_input, gate_input, mix_grad, conv_weight, step_raw.T, step_bias[None],
        rate_log[None], doc_ids.reshape(64, 128), input_coeff, output_coeff, queries, keys,
        values, attn_grad, skip_gain,
    )
    dconv, dgate, gstep, dw, sc, gin, gout, gq, gk, gv = finish(outs)
    return (
        gq, gk, gv, dconv, dgate, gstep.T, gin, gout, dw, sc[0, :NH], sc[1, :NH], sc[2, :NH]
    )


def solution(mesh):
    both = P("seq", "head")
    return jax.shard_map(
        local,
        mesh=mesh,
        in_specs=(
            both, both, both, both, P(), both, P(None, "head"), both, P("head"), P("head"),
            P("head"), P("seq", None), P("seq", None), both, both,
        ),
        out_specs=(
            both, both, both, both, both, both, P("seq", None), P("seq", None),
            P(None, "head"), P("head"), P("head"), P("head"),
        ),
        check_vma=False,
    )
```

time: 147 us -> 110 us (0.75)
  Pallas kernels: 127 us -> 107 us
  local copies, waits for them, and re-layouts: 14.8 us -> 1.31 us
  other arithmetic: 2.66 us -> 0 us
    pallas_call x3 -> x2, Pallas kernels: 127 us -> 107 us  [the longest x1 101 us: layer(): pl.pallas_call(layer_kernel, grid=(2 * PAIRS,), in_specs=[tok, tok, tok,...]
    unnamed x22 -> x0, local copies, waits for them, and re-layouts: 11.4 us -> none
where the time goes in v2:
time: 110 us; the launch traced here: 109 us
  Pallas kernels  107 us (97%)
  local copies, waits for them, and re-layouts  1.31 us (1%)
    pallas_call x1, Pallas kernels, layer(): pl.pallas_call(layer_kernel, grid=(2 * PAIRS,), in_specs=[tok, tok, tok,...  101 us
    pallas_call x1, Pallas kernels, finish(): pl.pallas_call(finish_kernel, grid=(parts,), in_specs=specs, out_specs=sp...  6.06 us

profile of v2, /device:TPU:0, one launch (start us, length us, event | category | flops | bytes accessed | tf_op | source)
XLA Modules:
  0.0 109.5 jit_solution(10314932541639048782)
XLA Ops:
  0.7 101.4 %layer.1 = (bf16[256,1792]{1,0:T(8,128)(2,1)}, bf16[256,1792]{1,0:T(8,128)(2,1)}, f32[28,256]{1,0:T(8,128)}, f32[4,1792]{1,0:T(4,128)}, f32[8,128]{1,0:T(8,128)}...) custom-call(bf16[256,1792]{1,0:T(8,128)(2,1)} %edge_ref.1, ...), custom_call_target="tpu_custom_call" | custom-call | flops 6000000000 | bytes 12000000 | tf_op jit(solution)/shard_map/layer/pallas_call | solution.py:669
  102.1 6.1 %finish.1 = (bf16[256,1792]{1,0:T(8,128)(2,1)}, bf16[256,1792]{1,0:T(8,128)(2,1)}, f32[28,256]{1,0:T(8,128)}, f32[4,1792]{1,0:T(4,128)}, f32[8,128]{1,0:T(8,128)...) custom-call(bf16[256,1792]{1,0:T(8,128)(2,1)} %get-tuple-element.32., ...), custom_call_target="tpu_custom_call" | custom-call | flops 1000000 | bytes 7000000 | tf_op jit(solution)/shard_map/finish/pallas_call | solution.py:774
  108.2 1.3 %slice_bitcast_fusion = (f32[28]{0:T(128)}, f32[28]{0:T(128)}, f32[28]{0:T(128)}) fusion(f32[8,128]{1,0:T(8,128)} %get-tuple-element.51), kind=kLoop, calls=%fused_computation | loop fusion | bytes 672 | tf_op jit(solution)/shard_map/squeeze | solution.py:797

commit v3 on v2

--- a/solution.py
+++ b/solution.py
@@ -130,13 +130,14 @@
     lax.fori_loop(1, NSEQ, greet, 0)
 
 
-def attention(x_me, kva, qda, drows, dka, dva, dq_out, send_dq):
+def attention(x_me, kva, qda, drows, dka, dva, dq_out, send_dq, midway):
     dka[...] = jnp.zeros_like(dka)
     dva[...] = jnp.zeros_like(dva)
     row_i = lax.broadcasted_iota(jnp.int32, (T, T), 0)
     col_j = lax.broadcasted_iota(jnp.int32, (T, T), 1)
 
     def chunk(c, carry):
+        pl.when(c == 2)(midway)
         slot = lax.rem(x_me - c + RING, RING)
         qt = qda[slot, 0]
         gt = qda[slot, 1]
@@ -196,7 +197,7 @@
     conv_ref, gate_ref, mix_ref, w_ref, raw_ref, bias_ref, rate_ref, doc_ref, bin_ref, cout_ref,
     q_ref, k_ref, v_ref, do_ref, edge_ref, skip_ref,
     dconv_out, dgate_out, step_out, dw_out, sc_out, gin_out, gout_out, gq_out, gk_out, gv_out,
-    drows, rows, tri, mk, vcol, small, xs, bg, cg, act_s, g_s,
+    drows, rows, tri, mk, vcol, small, xs, bg, cg, act_s, g_s, y_s, ds_s,
     kvp, qdp, tscr, kva, qda, tail_in, pay, inbox, outb, landed,
     dka, dva, dq_out, own_out, back_out, dq_in, own_in, back_in, fscr,
     bias_m, pair_t, dpair, dcum, ddir, dskp, dbt, dct, qs,
@@ -337,6 +338,9 @@
             return carry
 
         lax.fori_loop(1, NSEQ, send_first, 0)
+
+    @pl.when(step_id == 2 * PAIRS - 1)
+    def _():
         for k in range(1, RING):
             qd_copy(k).wait_recv()
         for k in range(RING):
@@ -347,43 +351,43 @@
             def _():
                 dq_copy(k).start()
 
-        attention(x_me, kva, qda, drows, dka, dva, dq_out, send_dq)
-
-        @pl.when(me < NH)
-        def _():
-            inbox[me] = pay[me]
-
-            def wait_first(k, carry):
-                first_copy(me, lax.rem(me + k, NSEQ)).wait_recv()
-                return carry
-
-            lax.fori_loop(1, NSEQ, wait_first, 0)
-            lane = lax.broadcasted_iota(jnp.int32, (64, 128), 1)
-
-            def gain(s):
-                tail = inbox[s, 64:80, :].astype(F32)
-                return tail[0:1] + tail[8:9]
-
-            def down(s, run):
-                outb[s] = run.astype(BF16)
-                return gain(s) * run + inbox[s, 0:64, :].astype(F32)
-
-            lax.fori_loop(0, NSEQ, down, jnp.zeros((64, 128), F32))
-
-            def up(k, run):
-                s = NSEQ - 1 - k
-                outb[s] = jnp.where(lane < STATE, outb[s].astype(F32), run).astype(BF16)
-                return gain(s) * run + inbox[s, 0:64, :].astype(F32)
-
-            lax.fori_loop(0, NSEQ, up, jnp.zeros((64, 128), F32))
-
-            def send_second(k, carry):
-                second_copy(lax.rem(me + k, NSEQ), me).start()
-                return carry
-
-            lax.fori_loop(1, NSEQ, send_second, 0)
-            landed[me] = outb[me]
-
+        def midway():
+            @pl.when(me < NH)
+            def _():
+                inbox[me] = pay[me]
+
+                def wait_first(k, carry):
+                    first_copy(me, lax.rem(me + k, NSEQ)).wait_recv()
+                    return carry
+
+                lax.fori_loop(1, NSEQ, wait_first, 0)
+                lane = lax.broadcasted_iota(jnp.int32, (64, 128), 1)
+
+                def gain(s):
+                    tail = inbox[s, 64:80, :].astype(F32)
+                    return tail[0:1] + tail[8:9]
+
+                def down(s, run):
+                    outb[s] = run.astype(BF16)
+                    return gain(s) * run + inbox[s, 0:64, :].astype(F32)
+
+                lax.fori_loop(0, NSEQ, down, jnp.zeros((64, 128), F32))
+
+                def up(k, run):
+                    s = NSEQ - 1 - k
+                    outb[s] = jnp.where(lane < STATE, outb[s].astype(F32), run).astype(BF16)
+                    return gain(s) * run + inbox[s, 0:64, :].astype(F32)
+
+                lax.fori_loop(0, NSEQ, up, jnp.zeros((64, 128), F32))
+
+                def send_second(k, carry):
+                    second_copy(lax.rem(me + k, NSEQ), me).start()
+                    return carry
+
+                lax.fori_loop(1, NSEQ, send_second, 0)
+                landed[me] = outb[me]
+
+        attention(x_me, kva, qda, drows, dka, dva, dq_out, send_dq, midway)
         for k in range(RING):
             c = lax.rem(x_me + k, RING)
             back_out[k, 0] = (dka[c] * SCALE).astype(BF16)
@@ -394,7 +398,7 @@
             if k:
                 own_copy(k).start()
 
-    @pl.when(step_id == PAIRS)
+    @pl.when(step_id == 2 * PAIRS)
     def _():
         def arrive(k, carry):
             peer = lax.rem(me + k, NSEQ)
@@ -407,25 +411,12 @@
 
         lax.fori_loop(1, NSEQ, arrive, 0)
 
-    @pl.when(step_id >= PAIRS)
+    @pl.when((step_id >= PAIRS) & (step_id < 2 * PAIRS))
     def _():
         act_t = act_s[rows128, :]
         g_t = g_s[rows128, :]
-        step_p = pair_rows(rows, 0, pair)
-        eg_p = pair_rows(rows, 3, pair)
-        te_p = pair_rows(rows, 4, pair)
-        s_t = act_t * step_p
-        s_b = s_t.astype(BF16)
+        s_b = (act_t * pair_rows(rows, 0, pair)).astype(BF16)
         g_b = g_t.astype(BF16)
-        state = jnp.concatenate([landed[2 * pair], landed[2 * pair + 1]], axis=0)
-        start = state[:, 0:STATE]
-        end = state[:, STATE:]
-        car = dot(start, cg[...], 1, 1) * eg_p
-        dste = dot(end, bg[...], 1, 1) * te_p
-        dct[...] += dot(start, (g_t * eg_p).astype(BF16), 0, 0)
-        dbt[...] += dot(end, (s_t * te_p).astype(BF16), 0, 0)
-        se = start.astype(F32) * end.astype(F32)
-        lane = lax.broadcasted_iota(jnp.int32, (1, T), 1)
         ys, dss = [], []
         for a in range(2):
             lo = 64 * a
@@ -438,32 +429,53 @@
             mb = m.astype(BF16)
             sh = s_b[lo : lo + 64]
             gh = g_b[lo : lo + 64]
-            y = dot(sh, mb, 1, 0)
+            ys.append(dot(sh, mb, 1, 0))
             dsi = dot(gh, mb, 1, 1)
+            dss.append(dsi)
             dm = dot(sh, gh, 0, 0)
             dpair[...] += dm * w
             z = dm * m
             zr = jnp.sum(jnp.transpose(z[:, 0:128] + z[:, 128:]), axis=0, keepdims=True)
-            carh = car[lo : lo + 64]
-            dsth = dste[lo : lo + 64]
-            gt = g_t[lo : lo + 64]
-            st = s_t[lo : lo + 64]
             at = act_t[lo : lo + 64]
-            v = jnp.sum(st * dsth, axis=0, keepdims=True)
-            d = jnp.sum(z, axis=0, keepdims=True) - zr + jnp.sum(gt * carh, axis=0, keepdims=True) - v
+            dcum[pl.ds(h, 1), :] = jnp.sum(z, axis=0, keepdims=True) - zr
+            ddir[pl.ds(h, 1), :] = jnp.sum(dsi * at, axis=0, keepdims=True)
+            dskp[pl.ds(h, 1), :] = jnp.sum(g_t[lo : lo + 64] * at, axis=0, keepdims=True)
+        y_s[rows128, :] = jnp.concatenate(ys, axis=0)
+        ds_s[rows128, :] = jnp.concatenate(dss, axis=0)
+
+    @pl.when(step_id >= 2 * PAIRS)
+    def _():
+        act_t = act_s[rows128, :]
+        g_t = g_s[rows128, :]
+        step_p = pair_rows(rows, 0, pair)
+        eg_p = pair_rows(rows, 3, pair)
+        te_p = pair_rows(rows, 4, pair)
+        s_t = act_t * step_p
+        state = jnp.concatenate([landed[2 * pair], landed[2 * pair + 1]], axis=0)
+        start = state[:, 0:STATE]
+        end = state[:, STATE:]
+        car = dot(start, cg[...], 1, 1) * eg_p
+        dste = dot(end, bg[...], 1, 1) * te_p
+        dct[...] += dot(start, (g_t * eg_p).astype(BF16), 0, 0)
+        dbt[...] += dot(end, (s_t * te_p).astype(BF16), 0, 0)
+        se = start.astype(F32) * end.astype(F32)
+        lane = lax.broadcasted_iota(jnp.int32, (1, T), 1)
+        skips = []
+        for a in range(2):
+            part = slice(64 * a, 64 * a + 64)
+            h = 2 * pair + a
+            v = jnp.sum(s_t[part] * dste[part], axis=0, keepdims=True)
+            d = jnp.sum(g_t[part] * car[part], axis=0, keepdims=True) - v
             thr = rows[3, pl.ds(h, 1), :][:, T - 1 : T]
             extra = jnp.sum(v, axis=1, keepdims=True) + thr * jnp.sum(
-                jnp.sum(se[lo : lo + 64], axis=0, keepdims=True), axis=1, keepdims=True
+                jnp.sum(se[part], axis=0, keepdims=True), axis=1, keepdims=True
             )
-            dcum[pl.ds(h, 1), :] = d + jnp.where(lane == T - 1, extra, 0.0)
-            ds = dsi + dsth
-            ddir[pl.ds(h, 1), :] = jnp.sum(ds * at, axis=0, keepdims=True)
-            dskp[pl.ds(h, 1), :] = jnp.sum(gt * at, axis=0, keepdims=True)
-            skip = skip_ref[h]
-            ys.append(y + carh + skip * at)
-            dss.append(ds * step_p[lo : lo + 64] + skip * gt)
-        y = jnp.transpose(jnp.concatenate(ys, axis=0))
-        dact = jnp.transpose(jnp.concatenate(dss, axis=0))
+            dcum[pl.ds(h, 1), :] += d + jnp.where(lane == T - 1, extra, 0.0)
+            ddir[pl.ds(h, 1), :] += jnp.sum(dste[part] * act_t[part], axis=0, keepdims=True)
+            skips.append(jnp.full((64, T), skip_ref[h], F32))
+        skip = jnp.concatenate(skips, axis=0)
+        y = jnp.transpose(y_s[rows128, :] + car + skip * act_t)
+        dact = jnp.transpose((ds_s[rows128, :] + dste) * step_p + skip * g_t)
         gate = gate_ref[...].astype(F32)
         sg = sigmoid(gate)
         dgate_out[...] = (
@@ -484,7 +496,7 @@
         dconv_out[:, rows128] = dx[8:].astype(BF16)
         last[:, rows128] = dx[T - 8 :]
 
-    @pl.when(step_id == 2 * PAIRS - 1)
+    @pl.when(step_id == 3 * PAIRS - 1)
     def _():
         dld = dot(dcum[...], tri[...], 1, 1, HI)
         rate = vcol[...]
@@ -663,12 +675,12 @@
         piece,
     ]
     specs = [whole_spec(o.shape) for o in outs]
-    specs[1] = pl.BlockSpec((T, 128), lambda i: (0, jnp.maximum(i - PAIRS, 0)))
+    specs[1] = pl.BlockSpec((T, 128), lambda i: (0, jnp.maximum(i - 2 * PAIRS, 0)))
     square = VM((T, T), F32)
     heads = VM((32, T), F32)
     return pl.pallas_call(
         layer_kernel,
-        grid=(2 * PAIRS,),
+        grid=(3 * PAIRS,),
         in_specs=[
             tok,
             tok,
@@ -698,6 +710,8 @@
             VM((8 + T, 128), F32),
             VM((T, STATE), BF16),
             VM((T, STATE), BF16),
+            VM((WIDTH, T), F32),
+            VM((WIDTH, T), F32),
             VM((WIDTH, T), F32),
             VM((WIDTH, T), F32),
             VM((RING, 2, HEAD_DIM, T), BF16),
@@ -757,9 +771,11 @@
 
 
 def finish_kernel(*refs):
-    half = len(refs) // 2
-    for src, dest in zip(refs[:half], refs[half:]):
+    count = (len(refs) - 4) // 2
+    for src, dest in zip(refs[:count], refs[count + 1 : 2 * count + 1]):
         dest[...] = src[...]
+    for i in range(3):
+        refs[2 * count + 1 + i][...] = refs[count][i : i + 1, 0:NH]
 
 
 def finish(arrays):
@@ -775,8 +791,9 @@
         finish_kernel,
         grid=(parts,),
         in_specs=specs,
-        out_specs=specs,
-        out_shape=[jax.ShapeDtypeStruct(a.shape, a.dtype) for a in arrays],
+        out_specs=specs[:-1] + [whole_spec((1, NH))] * 3,
+        out_shape=[jax.ShapeDtypeStruct(a.shape, a.dtype) for a in arrays[:-1]]
+        + [jax.ShapeDtypeStruct((1, NH), F32)] * 3,
         compiler_params=pltpu.CompilerParams(vmem_limit_bytes=60 * 1024 * 1024),
         name="finish",
         cost_estimate=pl.CostEstimate(flops=1000000, bytes_accessed=7000000, transcendentals=0),
@@ -792,9 +809,12 @@
         rate_log[None], doc_ids.reshape(64, 128), input_coeff, output_coeff, queries, keys,
         values, attn_grad, skip_gain,
     )
-    dconv, dgate, gstep, dw, sc, gin, gout, gq, gk, gv = finish(outs)
+    dconv, dgate, gstep, dw, gin, gout, gq, gk, gv, bias, rate, skip = finish(
+        outs[:4] + outs[5:] + outs[4:5]
+    )
     return (
-        gq, gk, gv, dconv, dgate, gstep.T, gin, gout, dw, sc[0, :NH], sc[1, :NH], sc[2, :NH]
+        gq, gk, gv, dconv, dgate, gstep.T, gin, gout, dw, bias.reshape(NH), rate.reshape(NH),
+        skip.reshape(NH),
     )
 
 

time: 110 us -> 106 us (0.964); the launches traced: 109 us -> 104 us
  Pallas kernels: 107 us -> 103 us
  local copies, waits for them, and re-layouts: 1.31 us -> 0 us
    pallas_call x1, Pallas kernels: 101 us -> 96.8 us  [layer(): pl.pallas_call(layer_kernel, grid=(3 * PAIRS,), in_specs=[tok, tok, tok,...]
    squeeze x1 -> x0, local copies, waits for them, and re-layouts: 1.31 us -> none  [local(): sc[2, :NH]]
where the time goes in v3:
time: 106 us; the launch traced here: 104 us
  Pallas kernels  103 us (97%)
    pallas_call x1, Pallas kernels, layer(): pl.pallas_call(layer_kernel, grid=(3 * PAIRS,), in_specs=[tok, tok, tok,...  96.8 us
    pallas_call x1, Pallas kernels, finish(): pl.pallas_call(finish_kernel, grid=(parts,), in_specs=specs, out_specs=sp...  6.09 us

profile of v3, /device:TPU:0, one launch (start us, length us, event | category | flops | bytes accessed | tf_op | source)
XLA Modules:
  0.0 103.6 jit_solution(12543542510773009948)
XLA Ops:
  0.7 96.8 %layer.1 = (bf16[256,1792]{1,0:T(8,128)(2,1)}, bf16[256,1792]{1,0:T(8,128)(2,1)}, f32[28,256]{1,0:T(8,128)}, f32[4,1792]{1,0:T(4,128)}, f32[8,128]{1,0:T(8,128)}...) custom-call(bf16[256,1792]{1,0:T(8,128)(2,1)} %edge_ref.1, ...), custom_call_target="tpu_custom_call" | custom-call | flops 6000000000 | bytes 12000000 | tf_op jit(solution)/shard_map/layer/pallas_call | solution.py:681
  97.5 6.1 %finish.1 = (bf16[256,1792]{1,0:T(8,128)(2,1)}, bf16[256,1792]{1,0:T(8,128)(2,1)}, f32[28,256]{1,0:T(8,128)}, f32[4,1792]{1,0:T(4,128)}, f32[256,128]{1,0:T(8,12...) custom-call(bf16[256,1792]{1,0:T(8,128)(2,1)} %get-tuple-element.34., ...), custom_call_target="tpu_custom_call" | custom-call | flops 1000000 | bytes 7000000 | tf_op jit(solution)/shard_map/finish/pallas_call | solution.py:790

commit v4 on v3

--- a/solution.py
+++ b/solution.py
@@ -145,7 +145,7 @@
         g = jnp.transpose(gt.astype(F32)).astype(BF16)
         dq_col = col_of(drows[pl.ds(RING + c, 1), :], 128)
         dq_col = jnp.concatenate([dq_col, dq_col], axis=1)
-        scores, masks, slots = [], [], []
+        scores, slots = [], []
         row_max = None
         for b in range(RING + 1):
             kc = c + b
@@ -158,12 +158,11 @@
                 ok = ok & (col_j <= row_i)
             s = jnp.where(ok, s, NEG)
             scores.append(s)
-            masks.append(ok)
             m = jnp.max(s, axis=1, keepdims=True)
             row_max = m if row_max is None else jnp.maximum(row_max, m)
         row_sum = None
         for b in range(RING + 1):
-            e = jnp.where(masks[b], jnp.exp(scores[b] - row_max), 0.0)
+            e = jnp.exp(scores[b] - row_max)
             scores[b] = e
             r = jnp.sum(e, axis=1, keepdims=True)
             row_sum = r if row_sum is None else row_sum + r
@@ -393,6 +392,8 @@
             back_out[k, 0] = (dka[c] * SCALE).astype(BF16)
             back_out[k, 1] = dva[c].astype(BF16)
             back_copy(k).start()
+        for k in range(RING):
+            c = lax.rem(x_me + k, RING)
             own_out[k, 0] = (dka[RING + c] * SCALE).astype(BF16)
             own_out[k, 1] = dva[RING + c].astype(BF16)
             if k:
@@ -553,8 +554,7 @@
                 dq_copy(k).wait_recv()
             h = lax.rem(x_me - k + RING, RING)
             source = dq_in if k else dq_out
-            fscr[pl.ds(pl.multiple_of(h * HEAD_DIM, 32), HEAD_DIM), :] = source[k].astype(F32)
-        gq_out[...] = jnp.transpose(fscr[...]).astype(BF16)
+            gq_out[pl.ds(pl.multiple_of(h * HEAD_DIM, 32), HEAD_DIM), :] = source[k]
         mine = me // 2
         owner = (me == 2 * mine) & (mine < BLOCKS)
 
@@ -593,10 +593,9 @@
             for k in range(RING):
                 mine_k = own_in if k else own_out
                 h = lax.rem(x_me - k + RING, RING)
-                fscr[pl.ds(pl.multiple_of(h * HEAD_DIM, 32), HEAD_DIM), :] = mine_k[
-                    k, slot
-                ].astype(F32) + back_in[k, slot].astype(F32)
-            dest[...] = jnp.transpose(fscr[...]).astype(BF16)
+                dest[pl.ds(pl.multiple_of(h * HEAD_DIM, 32), HEAD_DIM), :] = (
+                    mine_k[k, slot].astype(F32) + back_in[k, slot].astype(F32)
+                ).astype(BF16)
 
         def wait_second(b, carry):
             @pl.when(2 * b != me)
@@ -661,7 +660,7 @@
     queries, keys, values, attn_grad, skip,
 ):
     tok = pl.BlockSpec((T, 128), lambda i: (0, lax.rem(i, PAIRS)))
-    piece = jax.ShapeDtypeStruct((T, 4 * HEAD_DIM), BF16)
+    piece = jax.ShapeDtypeStruct((4 * HEAD_DIM, T), BF16)
     outs = [
         jax.ShapeDtypeStruct((T, WIDTH), BF16),
         jax.ShapeDtypeStruct((T, WIDTH), BF16),
@@ -732,7 +731,7 @@
             VM((RING, HEAD_DIM, T), BF16),
             VM((RING, 2, HEAD_DIM, T), BF16),
             VM((RING, 2, HEAD_DIM, T), BF16),
-            VM((4 * HEAD_DIM, T), F32),
+            VM((128, T), F32),
             square,
             square,
             square,
@@ -770,10 +769,16 @@
     )
 
 
+TURNED = (4 * HEAD_DIM, T)
+
+
 def finish_kernel(*refs):
     count = (len(refs) - 4) // 2
     for src, dest in zip(refs[:count], refs[count + 1 : 2 * count + 1]):
-        dest[...] = src[...]
+        if src.shape == dest.shape:
+            dest[...] = src[...]
+        else:
+            dest[...] = jnp.transpose(src[...].astype(F32)).astype(BF16)
     for i in range(3):
         refs[2 * count + 1 + i][...] = refs[count][i : i + 1, 0:NH]
 
@@ -781,19 +786,25 @@
 def finish(arrays):
     parts = 7
 
-    def spec(a):
-        if a.shape[0] == T and a.shape[1] > 128:
-            return pl.BlockSpec((T, a.shape[1] // parts), lambda i: (0, i))
+    def spec(a, turn):
+        if a.shape == TURNED:
+            if turn:
+                return pl.BlockSpec((T, a.shape[0] // parts), lambda i: (0, i))
+            return pl.BlockSpec((a.shape[0] // parts, T), lambda i: (i, 0))
+        if a.shape == (T, WIDTH):
+            return pl.BlockSpec((T, WIDTH // parts), lambda i: (0, i))
         return whole_spec(a.shape)
 
-    specs = [spec(a) for a in arrays]
+    def result(a):
+        shape = (T, 4 * HEAD_DIM) if a.shape == TURNED else a.shape
+        return jax.ShapeDtypeStruct(shape, a.dtype)
+
     return pl.pallas_call(
         finish_kernel,
         grid=(parts,),
-        in_specs=specs,
-        out_specs=specs[:-1] + [whole_spec((1, NH))] * 3,
-        out_shape=[jax.ShapeDtypeStruct(a.shape, a.dtype) for a in arrays[:-1]]
-        + [jax.ShapeDtypeStruct((1, NH), F32)] * 3,
+        in_specs=[spec(a, False) for a in arrays],
+        out_specs=[spec(a, True) for a in arrays[:-1]] + [whole_spec((1, NH))] * 3,
+        out_shape=[result(a) for a in arrays[:-1]] + [jax.ShapeDtypeStruct((1, NH), F32)] * 3,
         compiler_params=pltpu.CompilerParams(vmem_limit_bytes=60 * 1024 * 1024),
         name="finish",
         cost_estimate=pl.CostEstimate(flops=1000000, bytes_accessed=7000000, transcendentals=0),

time: 106 us -> 107 us (level)
  Pallas kernels: 103 us -> 105 us
    pallas_call x1, Pallas kernels: 96.8 us -> 98.5 us  [layer(): pl.pallas_call(layer_kernel, grid=(3 * PAIRS,), in_specs=[tok, tok, tok,...]
where the time goes in v4:
time: 107 us; the launch traced here: 105 us
  Pallas kernels  105 us (98%)
    pallas_call x1, Pallas kernels, layer(): pl.pallas_call(layer_kernel, grid=(3 * PAIRS,), in_specs=[tok, tok, tok,...  98.5 us
    pallas_call x1, Pallas kernels, finish(): pl.pallas_call(finish_kernel, grid=(parts,), in_specs=[spec(a, False) for...  6.24 us

profile of v4, /device:TPU:0, one launch (start us, length us, event | category | flops | bytes accessed | tf_op | source)
XLA Modules:
  0.0 105.4 jit_solution(17442917558988381368)
XLA Ops:
  0.7 98.5 %layer.1 = (bf16[256,1792]{1,0:T(8,128)(2,1)}, bf16[256,1792]{1,0:T(8,128)(2,1)}, f32[28,256]{1,0:T(8,128)}, f32[4,1792]{1,0:T(4,128)}, f32[8,128]{1,0:T(8,128)}...) custom-call(bf16[256,1792]{1,0:T(8,128)(2,1)} %edge_ref.1, ...), custom_call_target="tpu_custom_call" | custom-call | flops 6000000000 | bytes 12000000 | tf_op jit(solution)/shard_map/layer/pallas_call | solution.py:680
  99.2 6.2 %finish.1 = (bf16[256,1792]{1,0:T(8,128)(2,1)}, bf16[256,1792]{1,0:T(8,128)(2,1)}, f32[28,256]{1,0:T(8,128)}, f32[4,1792]{1,0:T(4,128)}, f32[256,128]{1,0:T(8,12...) custom-call(bf16[256,1792]{1,0:T(8,128)(2,1)} %get-tuple-element.34., ...), custom_call_target="tpu_custom_call" | custom-call | flops 1000000 | bytes 7000000 | tf_op jit(solution)/shard_map/finish/pallas_call | solution.py:802
